TPU v7x, 32 devices: a whole 2x2x4 slice. The times are simulated.
32 devices in a mesh: rep: 4 (over y, x), exp: 8 (over z, core).
Axes of the slice: x: 2, y: 2, z: 4, core: 2. Of those that a mesh axis runs over, the one named last changes fastest.
Arguments:
- tokens: bfloat16 [4096, 3584], P(('rep', 'exp')), parts along dimension 0, may hold values from -6 to 6
- expert_ids: int32 [4096, 4], P(('rep', 'exp')), parts along dimension 0, may hold values from 0 to 7, all different within a row; in each aligned block of 128 rows (0 to 127, 128 to 255, ...) at most 96 rows name the same one
- gate_probs: float32 [4096, 4], P(('rep', 'exp')), parts along dimension 0, may hold values from 0.1 to 1
- placed: int32 [8], replicated, may hold values from 0 to 7, each once
- w_gate: bfloat16 [8, 3584, 1024], P('exp'), may hold values from -0.09375 to 0.09375
- w_up: bfloat16 [8, 3584, 1024], P('exp'), may hold values from -0.09375 to 0.09375
- w_down: bfloat16 [8, 1024, 3584], P('exp'), may hold values from -0.1875 to 0.1875
Outputs:
- mixed: bfloat16 [4096, 3584], P(('rep', 'exp')), parts along dimension 0
There are 4 independent parts, one for each index of `rep`. A program takes and returns all parts, laid end to end along the dimension named above; an argument that names none is the same for every part. Nothing has to cross between parts.
Inputs may be any that keep to these rules, and one draw needn't show every extreme that they name: `expert_ids`: each row names 4 different experts. In the rows of one device no expert is named more than 96 times, a bound that some block reaches. `placed`: each expert once.
All inputs are finite; a program needn't handle non-finite values.
Results may differ from a plain program's by a relative error of at most 0.008.
Values may be sent and summed in bfloat16 or wider, within the bound.
No kernel may reach another device: no remote copies, remote signals or barrier semaphores. Data moves between devices by JAX's collectives and lax.ppermute only.
A program may use at most 192 MiB of HBM per device.

v0:
```python
import jax
import jax.numpy as jnp
from jax import lax
from jax.sharding import PartitionSpec as P

TOK_DEV = 128


def expert_rows(rows, gate_w, up_w, down_w):
    gate = jnp.dot(rows, gate_w, preferred_element_type=jnp.float32)
    up = jnp.dot(rows, up_w, preferred_element_type=jnp.float32)
    hidden = (jax.nn.silu(gate) * up).astype(jnp.bfloat16)
    return jnp.dot(hidden, down_w, preferred_element_type=jnp.float32).astype(jnp.bfloat16)


def run_expert(received, gate_w, up_w, down_w):
    sources, room, width = received.shape
    total_rows = sources * room
    flat = received.reshape(total_rows, width)
    result = expert_rows(flat, gate_w, up_w, down_w)
    return result.reshape(sources, room, width)


def body(tokens, expert_ids, gate_probs, placed, w_gate, w_up, w_down):
    tok_rows, width = tokens.shape
    picks = expert_ids.shape[1]
    devices = lax.axis_size("exp")
    average = tok_rows * picks // devices
    room = average + max(1, tok_rows * picks // (2 * devices))
    here = lax.axis_index("exp")
    mine = placed[here]
    gate_w, up_w, down_w = (w_gate[0], w_up[0], w_down[0])
    numbers = jnp.arange(devices, dtype=jnp.int32)
    home = jnp.sum(jnp.where(placed[None, :] == numbers[:, None], numbers[None, :], 0), axis=1)
    flat_ids = expert_ids.reshape(-1)
    target_dev = jnp.take(home, flat_ids)
    one_hot = (target_dev[:, None] == numbers[None, :]).astype(jnp.int32)
    rank = jnp.sum((jnp.cumsum(one_hot, axis=0) - 1) * one_hot, axis=1)
    slot_index = target_dev * room + rank
    rows_x = lax.all_gather(tokens, "exp", axis=0, tiled=True)
    rows_ids = lax.all_gather(expert_ids.astype(jnp.bfloat16), "exp", axis=0, tiled=True)
    shards = rows_x.shape[0] // TOK_DEV
    match = rows_ids.astype(jnp.int32).reshape(shards, TOK_DEV * picks) == mine
    order = jnp.cumsum(match.astype(jnp.int32), axis=1) - 1
    spot = jnp.where(match, order, room)
    within = jnp.broadcast_to(
        (jnp.arange(TOK_DEV * picks, dtype=jnp.int32) // picks)[None, :], (shards, TOK_DEV * picks)
    )
    shard_num = jnp.broadcast_to(
        jnp.arange(shards, dtype=jnp.int32)[:, None], (shards, TOK_DEV * picks)
    )
    slot_tok = (
        jnp.full((shards, room), TOK_DEV, jnp.int32).at[shard_num, spot].set(within, mode="drop")
    )
    global_row = jnp.where(
        slot_tok < TOK_DEV,
        jnp.arange(shards, dtype=jnp.int32)[:, None] * TOK_DEV + slot_tok,
        shards * TOK_DEV,
    )
    got = jnp.take(rows_x, global_row.reshape(-1), axis=0, mode="fill", fill_value=0)
    got = got.reshape(shards, room, width)
    counts = jnp.sum(match, axis=1)
    received, counts = (got, counts)
    produced = run_expert(received, gate_w, up_w, down_w)
    returned = lax.all_to_all(produced, "exp", split_axis=0, concat_axis=0, tiled=True)
    picked = jnp.take(returned.reshape(devices * room, width), slot_index, axis=0)
    picked = picked.reshape(tok_rows, picks, width)
    mixed = jnp.einsum("tk,tkd->td", gate_probs, picked.astype(jnp.float32))
    return mixed.astype(jnp.bfloat16)


def solution(mesh):
    return jax.shard_map(
        body,
        mesh=mesh,
        in_specs=(
            P(("rep", "exp"), None),
            P(("rep", "exp"), None),
            P(("rep", "exp"), None),
            P(),
            P("exp", None, None),
            P("exp", None, None),
            P("exp", None, None),
        ),
        out_specs=P(("rep", "exp"), None),
        check_vma=False,
    )
```

profile of v0, /device:TPU:0, one launch (start us, length us, event | category | flops | bytes accessed | tf_op | source)
XLA Modules:
  0.0 287.1 jit_solution(18325385984931404758)
XLA Ops:
  6.5 0.7 all-gather.2.cloned.1.call-update
  7.3 0.7 convert_element_type.29
  7.9 1.2 dynamic_slice.3
  9.2 13.5 %all_gather.6 = bf16[1024,4]{0,1:T(4,128)(2,1)S(1)} all-gather(bf16[128,4]{0,1:T(4,128)(2,1)S(1)} %convert_element_type.29), channel_id=1, replica_groups=mesh['rep'=4,'exp'=8] {'exp'}, dimensions={0}, use_global_device_ids=true | all-gather | bytes 9216 | tf_op jit(solution)/shard_map/all_gather | solution.py:41
  22.6 0.7 fusion.31
  23.8 1.1 reduce-window.16
  25.5 0.4 eq.63
  26.0 0.7 multiply_reduce_fusion
  26.7 0.7 and_reduce_fusion
  27.5 15.7 %scatter_custom_fusion = s32[768]{0:T(1024)S(1)} fusion(s32[4096]{0:T(1024)S(1)} %bitcast.56, s32[4096]{0:T(1024)S(1)} %bitcast.57, s32[]{:T(128)} %constant.84.clone.1), kind=kCustom, calls=%fused_computation.63 | custom fusion | bytes 3076
  43.6 41.5 %all-gather.2.cloned.1.call-done = bf16[1024,3584]{1,0:T(8,128)(2,1)} async-done(((bf16[128,3584]{1,0:T(8,128)(2,1)}), bf16[1024,3584]{1,0:T(8,128)(2,1)}) %all-gather.2.cloned.1.call-update) | async-done | bytes 7340048 | tf_op jit(solution)/shard_map/all_gather | solution.py:40
  85.1 15.0 %gather_fusion = bf16[768,3584]{1,0:T(8,128)(2,1)} fusion(bf16[1024,3584]{1,0:T(8,128)(2,1)} %all-gather.2.cloned.1.call-done, s32[1024]{0:T(1024)S(1)} %pad_clamp_fusion.1), kind=kCustom, calls=%fused_computation | custom fusion | bytes 11013120 | tf_op jit(solution)/shard_map/jit(_take)/gather | solution.py:60
  100.1 9.8 %fusion.2 = f32[768,1024]{1,0:T(8,128)S(1)} fusion(bf16[1,3584,1024]{2,1,0:T(8,128)(2,1)} %param.12, bf16[768,3584]{1,0:T(8,128)(2,1)} %gather_fusion, pred[768]{0:T(1024)(128)(4,1)S(1)} %compare_and_fusion), kind=kOutput, calls=%fused_computation.5 | convolution fusion | flops 5639897088 | bytes 15991552 | tf_op jit(solution)/shard_map/dot_general | solution.py:11
  109.9 19.9 %fusion.6 = bf16[768,3584]{1,0:T(8,128)(2,1)} fusion(bf16[1,1024,3584]{2,1,0:T(8,128)(2,1)} %param.13, f32[768,1024]{1,0:T(8,128)S(1)} %fusion.2, bf16[1,3584,1024]{2,1,0:T(8,128)(2,1)} %param.11, bf16[768,3584]{1,0:T(8,128)(2,1)} %gather_fusion, pred[768]{0:T(1024)(128)(4,1)S(1)} %compare_and_fusion), kind=kOutput, calls=%fused_computation.9 | convolution fusion | flops 11284512768 | bytes 28836608 | tf_op jit(solution)/shard_map/dot_general | solution.py:13
  129.9 5.0 %all-to-all-start = ((bf16[8,96,3584]{2,1,0:T(8,128)(2,1)}), bf16[8,96,3584]{2,1,0:T(8,128)(2,1)}, u32[]{:S(2)}, u32[]{:S(2)}) async-start(bf16[8,96,3584]{2,1,0:T(8,128)(2,1)} %bitcast.53), calls=%async_computation | async-start | bytes 11010048 | tf_op jit(solution)/shard_map/all_to_all | solution.py:65
  135.5 0.7 fusion.32
  136.2 4.3 %compare_select_fusion.5 = s32[512,1]{0,1:T(1,128)S(1)} fusion(s32[]{:T(128)} %bitcast.1, s32[]{:T(128)} %bitcast.2, s32[]{:T(128)} %bitcast.3, s32[]{:T(128)} %bitcast.4, s32[]{:T(128)} %bitcast.5, s32[]{:T(128)} %bitcast.7, s32[]{:T(128)} %bitcast.6, s32[512,1]{0,1:T(1,128)S(1)} %reshape.270), kind=kLoop, calls=%fused_computation.38 | loop fusion | flops 7680 | bytes 4124 | tf_op jit(solution)/shard_map/jit(_take)/gather | solution.py:36
  140.4 0.7 and_select_fusion.1
  141.2 1.1 reduce-window.14
  143.4 113.4 %all-to-all-done = bf16[8,96,3584]{2,1,0:T(8,128)(2,1)} async-done(((bf16[8,96,3584]{2,1,0:T(8,128)(2,1)}), bf16[8,96,3584]{2,1,0:T(8,128)(2,1)}, u32[]{:S(2)}, u32[]{:S(2)}) %all-to-all-start) | async-done | bytes 5505056 | tf_op jit(solution)/shard_map/all_to_all | solution.py:65
  256.7 11.2 %gather_fusion.1 = bf16[512,3584]{1,0:T(8,128)(2,1)} fusion(bf16[768,3584]{1,0:T(8,128)(2,1)} %bitcast.18, s32[1024]{0:T(1024)S(1)} %pad_clamp_fusion), kind=kCustom, calls=%fused_computation.1 | custom fusion | bytes 7342080 | tf_op jit(solution)/shard_map/jit(_take)/gather | solution.py:66
  268.0 7.0 %gather.26 = bf16[128,4,3584]{2,1,0:T(4,128)(2,1)} reshape(bf16[512,3584]{1,0:T(8,128)(2,1)} %gather_fusion.1) | data formatting | bytes 7340032 | tf_op jit(solution)/shard_map/jit(_take)/gather | solution.py:66
  275.0 4.2 %fusion.9 = bf16[128,1,3584]{2,1,0:T(2,128)(2,1)S(1)} fusion(bf16[128,4,1]{1,2,0:T(2,128)(2,1)S(1)} %copy.40, bf16[128,4,3584]{2,1,0:T(4,128)(2,1)} %gather.26, pred[128,4]{1,0:T(8,128)(4,1)S(1)} %copy.36), kind=kOutput, calls=%fused_computation.11 | convolution fusion | flops 5505024 | bytes 4589056 | tf_op jit(solution)/shard_map/tk,tkd->td/dot_general | solution.py:68
  279.2 1.0 copy.45
  (50 shorter events, 3.2 us)
Async XLA Ops:
  6.5 78.6 %all-gather.2.cloned.1.call-start = ((), (), s32[]{:S(2)}) async-start(), calls=%async_computation.1 | async-start | bytes 8257536 | tf_op jit(solution)/shard_map/all_gather | solution.py:40
  129.8 5.1 %copy-start = (s32[128,4]{0,1:T(4,128)S(1)}, s32[128,4]{0,1:T(4,128)}, u32[]{:S(2)}) copy-start(s32[128,4]{0,1:T(4,128)} %param.8) | copy-start | bytes 6148
  129.8 5.5 %copy-start.2 = (s32[8]{0:T(128)S(1)}, s32[8]{0:T(128)}, u32[]{:S(2)}) copy-start(s32[8]{0:T(128)} %param.10) | copy-start | bytes 100
  129.8 13.3 %copy-start.1 = (f32[128,4]{0,1:T(4,128)S(1)}, f32[128,4]{0,1:T(4,128)}, u32[]{:S(2)}) copy-start(f32[128,4]{0,1:T(4,128)} %param.9) | copy-start | bytes 6148
  129.9 126.9 %all-to-all-start = ((bf16[8,96,3584]{2,1,0:T(8,128)(2,1)}), bf16[8,96,3584]{2,1,0:T(8,128)(2,1)}, u32[]{:S(2)}, u32[]{:S(2)}) async-start(bf16[8,96,3584]{2,1,0:T(8,128)(2,1)} %bitcast.53), calls=%async_computation | async-start | bytes 11010048 | tf_op jit(solution)/shard_map/all_to_all | solution.py:65
Sparse Core Ops, SparseCore 0:
  9.0 76.0 all-gather.1
where the time goes:
time: 288 us; the launch traced here: 287 us
  waiting for transfers between devices  156 us (54%)
  local copies, waits for them, and re-layouts  54.8 us (19%)
  matrix products  33.9 us (12%)
  between operations  13.6 us (5%)
  blocking collectives  13.5 us (5%)
  other arithmetic  10.6 us (4%)
  starting transfers between devices  5.04 us (2%)
    all_to_all x1, waiting for transfers between devices, body(): lax.all_to_all(produced, 'exp', split_axis=0, concat_axis=0, tiled=True)  113 us
    all_gather x1, waiting for transfers between devices, body(): rows_x = lax.all_gather(tokens, 'exp', axis=0, tiled=True)  41.5 us
    dot_general x1, matrix products, expert_rows(): jnp.dot(hidden, down_w, preferred_element_type=jnp.float32)  19.9 us
    gather x2, local copies, waits for them, and re-layouts, body(): jnp.take(returned.reshape(devices * room, width), slot_index, axis=0)  18.3 us
    unnamed x12, local copies, waits for them, and re-layouts  16 us
    gather x1, local copies, waits for them, and re-layouts, body(): jnp.take(rows_x, global_row.reshape(-1), axis=0, mode='fill', fill_value=0)  15 us
    all_gather x1, blocking collectives, body(): lax.all_gather(expert_ids.astype(jnp.bfloat16), 'exp', axis=0, tiled=True)  13.5 us
    dot_general x1, matrix products, expert_rows(): up = jnp.dot(rows, up_w, preferred_element_type=jnp.float32)  9.8 us
  transfers between devices with their start and end apart: 2, of which 2 were waited for; matrix products, arithmetic and copies ran while one was open for 11% of the time, Pallas kernels for 0%

commit v1 on v0

--- a/solution.py
+++ b/solution.py
@@ -1,9 +1,16 @@
+import functools
 import jax
 import jax.numpy as jnp
 from jax import lax
+from jax.experimental import pallas as pl
+from jax.experimental.pallas import tpu as pltpu
 from jax.sharding import PartitionSpec as P
 
+
 TOK_DEV = 128
+CORES = 2
+LINE = 4
+LANES = 128
 
 
 def expert_rows(rows, gate_w, up_w, down_w):
@@ -21,7 +28,7 @@
     return result.reshape(sources, room, width)
 
 
-def body(tokens, expert_ids, gate_probs, placed, w_gate, w_up, w_down):
+def sparse_body(tokens, expert_ids, gate_probs, placed, w_gate, w_up, w_down):
     tok_rows, width = tokens.shape
     picks = expert_ids.shape[1]
     devices = lax.axis_size("exp")
@@ -60,13 +67,341 @@
     got = jnp.take(rows_x, global_row.reshape(-1), axis=0, mode="fill", fill_value=0)
     got = got.reshape(shards, room, width)
     counts = jnp.sum(match, axis=1)
-    received, counts = (got, counts)
+    received = got
     produced = run_expert(received, gate_w, up_w, down_w)
     returned = lax.all_to_all(produced, "exp", split_axis=0, concat_axis=0, tiled=True)
     picked = jnp.take(returned.reshape(devices * room, width), slot_index, axis=0)
     picked = picked.reshape(tok_rows, picks, width)
     mixed = jnp.einsum("tk,tkd->td", gate_probs, picked.astype(jnp.float32))
     return mixed.astype(jnp.bfloat16)
+
+
+def run_kernel(width, devices, spot, block, twin, gate_w, up_w, down_w, own, other, rows):
+    half = own.shape[0]
+    rows[:half] = block[...]
+    rows[half:] = twin[...]
+    lane = lax.broadcasted_iota(jnp.int32, (2 * half, LANES), 1)
+    mine = (lane == spot[0]) | (lane == spot[0] + devices)
+    weights = rows[:, width:].astype(jnp.float32)
+    scale = jnp.sum(jnp.where(mine, weights, 0.0), axis=1, keepdims=True)
+    x = rows[:, :width]
+    gate = jnp.dot(x, gate_w[...], preferred_element_type=jnp.float32)
+    up = jnp.dot(x, up_w[...], preferred_element_type=jnp.float32)
+    hidden = (gate / (1.0 + jnp.exp(-gate)) * up).astype(jnp.bfloat16)
+    result = jnp.dot(hidden, down_w[...], preferred_element_type=jnp.float32) * scale
+    own[...] = result[:half]
+    other[...] = result[half:].astype(jnp.bfloat16)
+
+
+def at_end(spot):
+    return (spot[0] < CORES) | (spot[0] >= CORES * (LINE - 1))
+
+
+def load_kernel(source, after, held, sem):
+    copy = pltpu.make_async_copy(source.at[0], held, sem)
+    copy.start()
+    copy.wait()
+
+
+def prepare_kernel(devices, placed_hbm, tokens_hbm, ids_hbm, probs_hbm, *refs):
+    outs, (placed, tokens, ids, probs, sems) = refs[:5], refs[5:]
+    rows, width = tokens.shape
+    copies = [
+        pltpu.make_async_copy(src, dst, sems.at[n])
+        for n, (src, dst) in enumerate(
+            ((placed_hbm, placed), (ids_hbm, ids), (probs_hbm, probs), (tokens_hbm, tokens))
+        )
+    ]
+    for copy in copies:
+        copy.start()
+    for copy in copies[:3]:
+        copy.wait()
+    slot = lax.broadcasted_iota(jnp.int32, (LANES, rows), 0)
+    weight = jnp.zeros((LANES, rows), jnp.float32)
+    for s in range(devices):
+        total = jnp.zeros((1, rows), jnp.float32)
+        for k in range(ids.shape[0]):
+            total += jnp.where(ids[k : k + 1, :] == placed[s], probs[k : k + 1, :], 0.0)
+        high = total.astype(jnp.bfloat16).astype(jnp.float32)
+        weight = jnp.where(slot == s, high, jnp.where(slot == s + devices, total - high, weight))
+    packed = weight.T.astype(jnp.bfloat16)
+    copies[3].wait()
+    start = 0
+    for out in outs[:-1]:
+        size = out.shape[0]
+        out[:, :width] = tokens[start : start + size, :]
+        out[:, width:] = packed[start : start + size, :]
+        start += size
+    outs[-1][:, :width] = tokens[...]
+    outs[-1][:, width:] = packed
+
+
+def gate_kernel(before, out):
+    out[...] = before[...]
+
+
+def join_kernel(spot, outer_x, outer_y, inner_x, inner_y, gate, out):
+    part = outer_x.shape[0]
+
+    @pl.when(at_end(spot))
+    def _():
+        out[:part] = outer_x[...]
+        out[part:] = outer_y[...]
+
+    @pl.when(jnp.logical_not(at_end(spot)))
+    def _():
+        out[:part] = inner_x[...]
+        out[part:] = inner_y[...]
+
+
+def over_kernel(start, spot, own, back, passed, out):
+    part, width = out.shape[0], own.shape[1]
+
+    @pl.when(at_end(spot))
+    def _():
+        total = own[start : start + part] + back[start : start + part].astype(jnp.float32)
+        out[:, :width] = total.astype(out.dtype)
+        out[:, width:] = jnp.zeros((part, out.shape[1] - width), out.dtype)
+
+    @pl.when(jnp.logical_not(at_end(spot)))
+    def _():
+        out[...] = passed[...]
+
+
+def pass_kernel(spot, mine, passed, out):
+    @pl.when(at_end(spot))
+    def _():
+        out[...] = mine[...]
+
+    @pl.when(jnp.logical_not(at_end(spot)))
+    def _():
+        out[...] = passed[...]
+
+
+def add_kernel(start, spot, own, back, other, out):
+    part, width = out.shape
+    total = own[start : start + part] + back[start : start + part].astype(jnp.float32)
+    out[...] = (total + other[:, :width].astype(jnp.float32)).astype(out.dtype)
+
+
+def ends_kernel(start, spot, outer_own, outer_back, inner_own, inner_back, other, out):
+    part = out.shape[0]
+
+    @pl.when(at_end(spot))
+    def _():
+        total = outer_own[start : start + part] + outer_back[start : start + part].astype(jnp.float32)
+        out[...] = total.astype(out.dtype)
+
+    @pl.when(jnp.logical_not(at_end(spot)))
+    def _():
+        total = inner_own[start : start + part] + inner_back[start : start + part].astype(jnp.float32)
+        out[...] = (total + other[...].astype(jnp.float32)).astype(out.dtype)
+
+
+def finish_kernel(spot, own, back, *refs):
+    out = refs[-1]
+    part, width = refs[0].shape
+    for n in range(4):
+        sums, near, far = refs[3 * n : 3 * n + 3]
+        rows = slice(n * part, (n + 1) * part)
+        total = own[rows] + back[rows].astype(jnp.float32)
+
+        @pl.when(at_end(spot))
+        def _():
+            out[rows] = (total + sums[...].astype(jnp.float32)).astype(out.dtype)
+
+        @pl.when(jnp.logical_not(at_end(spot)))
+        def _():
+            both = near[:, :width].astype(jnp.float32) + far[...].astype(jnp.float32)
+            out[rows] = (total + both).astype(out.dtype)
+
+
+def line_body(tokens, expert_ids, gate_probs, placed, w_gate, w_up, w_down):
+    tok_rows, width = tokens.shape
+    devices = lax.axis_size("exp")
+    here = lax.axis_index("exp")
+    last = devices // CORES - 1
+    half = tok_rows // 2
+    part = half // 2
+    spot = here.reshape(1).astype(jnp.int32)
+    vmem = pl.BlockSpec(memory_space=pltpu.VMEM)
+    smem = pl.BlockSpec(memory_space=pltpu.SMEM)
+
+    def small(kernel, shape, *operands, extra=()):
+        return pl.pallas_call(
+            kernel,
+            in_specs=[smem] + [vmem] * (len(operands) + len(extra)),
+            out_specs=vmem,
+            out_shape=jax.ShapeDtypeStruct(shape, jnp.bfloat16),
+            cost_estimate=pl.CostEstimate(flops=shape[0] * shape[1] * 100, bytes_accessed=0, transcendentals=0),
+            compiler_params=pltpu.CompilerParams(vmem_limit_bytes=8 << 20),
+        )(spot, *operands, *extra)
+
+    def spread(pairs):
+        return [(CORES * a + c, CORES * b + c) for a, b in pairs for c in range(CORES)]
+
+    pair = spread([(0, 1), (1, 0), (last - 1, last), (last, last - 1)])
+    twins = [(i, i ^ 1) for i in range(devices)]
+    ends = (0, 1, devices - 2, devices - 1)
+    middle = spread([(1, 2), (2, 1)]) + [(i, i ^ 1) for i in ends]
+
+    def send(value, perm):
+        return lax.ppermute(value, "exp", perm)
+
+    long = width + LANES
+    given = [pltpu.with_memory_space_constraint(v, pltpu.HBM) for v in (placed, tokens, expert_ids.T, gate_probs.T)]
+    pieces = pl.pallas_call(
+        functools.partial(prepare_kernel, devices),
+        in_specs=[pl.BlockSpec(memory_space=pltpu.HBM)] * 4,
+        out_specs=[vmem] * 5,
+        out_shape=[jax.ShapeDtypeStruct((n, long), jnp.bfloat16) for n in (part,) * 4 + (tok_rows,)],
+        scratch_shapes=[pltpu.SMEM(placed.shape, placed.dtype)]
+        + [pltpu.VMEM(v.shape, v.dtype) for v in given[1:]]
+        + [pltpu.SemaphoreType.DMA((4,))],
+        compiler_params=pltpu.CompilerParams(vmem_limit_bytes=8 << 20),
+    )(*given)
+    own_a, own_b, own = pieces[:2], pieces[2:4], pieces[4]
+
+    def load(source, after):
+        return pl.pallas_call(
+            load_kernel,
+            in_specs=[pl.BlockSpec(memory_space=pltpu.HBM), pl.BlockSpec(memory_space=pl.ANY)],
+            out_specs=vmem,
+            out_shape=pltpu.VMEM(source.shape[1:], source.dtype),
+            scratch_shapes=[pltpu.SemaphoreType.DMA],
+            cost_estimate=pl.CostEstimate(flops=source.size * 200, bytes_accessed=0, transcendentals=0),
+            compiler_params=pltpu.CompilerParams(vmem_limit_bytes=1 << 20),
+        )(pltpu.with_memory_space_constraint(source, pltpu.HBM), after)
+
+    held = [load(w, own) for w in (w_gate, w_up, w_down)]
+
+    def run(block, twin=None):
+        count = block.shape[0]
+        if twin is None:
+            twin = send(block, twins)
+        call = pl.pallas_call(
+            functools.partial(run_kernel, width, devices),
+            in_specs=[smem] + [vmem] * 5,
+            out_specs=[vmem, vmem],
+            out_shape=[
+                jax.ShapeDtypeStruct((count, width), jnp.float32),
+                jax.ShapeDtypeStruct((count, width), jnp.bfloat16),
+            ],
+            scratch_shapes=[pltpu.VMEM((2 * count, long), jnp.bfloat16)],
+            cost_estimate=pl.CostEstimate(
+                flops=count * width * w_gate.shape[2] * 3, bytes_accessed=0, transcendentals=0
+            ),
+            compiler_params=pltpu.CompilerParams(vmem_limit_bytes=count * (160 << 10)),
+        )
+        mine, other = call(spot, block, twin, *held)
+        return mine, send(other, twins)
+
+    g = [[None, None] for _ in range(8)]
+    m = [[None, None] for _ in range(8)]
+    near_a = mid_a = far_a = far_b = mid_b = near_b = None
+
+    def start(slot, n):
+        first = n * part
+
+        def over(sums, passed):
+            return small(functools.partial(over_kernel, first), (part, long), *sums, passed)
+
+        def between(sums, other):
+            return small(functools.partial(add_kernel, first), (part, width), *sums, other)
+
+        def ends(outer_sums, inner_sums, other):
+            kernel = functools.partial(ends_kernel, first)
+            return small(kernel, (part, width), *outer_sums, *inner_sums, other)
+
+        if slot == 0:
+            pair_rows, middle_rows = own_a[n], own_a[n]
+        elif slot == 1:
+            pair_rows = small(pass_kernel, (part, long), own_b[n], m[0][n])
+            middle_rows = g[0][n]
+        elif slot == 2:
+            pair_rows, middle_rows = over(near_a, m[1][n]), g[1][n]
+        elif slot == 3:
+            pair_rows, middle_rows = over(mid_a, m[2][n]), own_b[n]
+        elif slot == 4:
+            pair_rows, middle_rows = over(far_a, m[3][n]), between(mid_a, g[3][n])
+        elif slot == 5:
+            pair_rows, middle_rows = over(far_b, own_b[n]), between(far_a, g[4][n])
+        elif slot == 6:
+            pair_rows, middle_rows = ends(mid_b, near_a, m[5][n]), between(far_b, g[5][n])
+        else:
+            pair_rows, middle_rows = ends(near_b, near_b, m[6][n]), between(mid_b, g[6][n])
+        g[slot][n] = send(pair_rows, pair)
+        m[slot][n] = send(middle_rows, middle)
+
+    def after(slot, n, result):
+        g[slot][n], m[slot][n], result = lax.optimization_barrier((g[slot][n], m[slot][n], result))
+        return result
+
+    def block(outer_rows, inner_rows):
+        return small(join_kernel, (half, long), *outer_rows, *inner_rows, extra=(gates[-1],))
+
+    gates = [jnp.zeros((8, LANES), jnp.int32)]
+
+    def gate():
+        call = pl.pallas_call(
+            gate_kernel,
+            in_specs=[vmem],
+            out_specs=vmem,
+            out_shape=jax.ShapeDtypeStruct((8, LANES), jnp.int32),
+            compiler_params=pltpu.CompilerParams(vmem_limit_bytes=1 << 20),
+        )
+        gates.append(call(gates[-1]))
+
+    start(0, 0)
+    start(0, 1)
+    after(0, 0, ())
+    start(1, 0)
+    gate()
+    after(0, 1, ())
+    start(1, 1)
+    near_a = after(1, 0, run(block(g[0], g[0])))
+    start(2, 0)
+    gate()
+    after(1, 1, ())
+    start(2, 1)
+    mid_a = after(2, 0, run(block(g[1], m[0])))
+    start(3, 0)
+    gate()
+    after(2, 1, ())
+    start(3, 1)
+    far_a = after(3, 0, run(block(g[2], m[1])))
+    start(4, 0)
+    gate()
+    after(3, 1, ())
+    start(4, 1)
+    far_b = after(4, 0, run(block(g[3], m[2])))
+    start(5, 0)
+    gate()
+    after(4, 1, ())
+    start(5, 1)
+    mid_b = after(5, 0, run(block(g[4], m[3])))
+    start(6, 0)
+    gate()
+    after(5, 1, ())
+    start(6, 1)
+    near_b = after(6, 0, run(block(g[5], g[1])))
+    start(7, 0)
+    gate()
+    after(6, 1, ())
+    start(7, 1)
+    mine, back = run(own)
+    ends = []
+    for n in range(2):
+        ends += [g[6][n], g[2][n], m[4][n]]
+    for n in range(2):
+        ends += [g[7][n], g[7][n], m[7][n]]
+    return small(finish_kernel, (tok_rows, width), mine, back, *ends, extra=(gates[-1],))
+
+
+def body(tokens, *rest):
+    if lax.axis_size("exp") == CORES * LINE:
+        return line_body(tokens, *rest)
+    return sparse_body(tokens, *rest)
 
 
 def solution(mesh):

time: 288 us -> 160 us (0.56)
  waiting for transfers between devices: 156 us -> 89.7 us
  local copies, waits for them, and re-layouts: 54.8 us -> 0.01 us
  Pallas kernels: 0 us -> 38.9 us
  matrix products: 33.9 us -> 0 us
  starting transfers between devices: 5.04 us -> 30.6 us
  blocking collectives: 13.5 us -> 0 us
  between operations: 13.6 us -> 0.5 us
  other arithmetic: 10.6 us -> 0 us
    all_to_all x1 -> x0, waiting for transfers between devices: 113 us -> none  [body(): lax.all_to_all(produced, 'exp', split_axis=0, concat_axis=0, tiled=True)]
    ppermute x0 -> x46, waiting for transfers between devices: none -> 89.7 us  [send(): return lax.ppermute(value, 'exp', perm)]
    all_gather x1 -> x0, waiting for transfers between devices: 41.5 us -> none  [body(): rows_x = lax.all_gather(tokens, 'exp', axis=0, tiled=True)]
    pallas_call x0 -> x47, Pallas kernels: none -> 38.9 us  [the longest x7 24.8 us: run(): mine, other = call(spot, block, twin, *held)]
    gather x6 -> x0, local copies, waits for them, and re-layouts: 34.1 us -> none  [the longest x2 18.3 us: body(): jnp.take(returned.reshape(devices * room, width), slot_index, axis=0)]
    dot_general x3 -> x0, matrix products: 33.9 us -> none  [the longest x1 19.9 us: expert_rows(): jnp.dot(hidden, down_w, preferred_element_type=jnp.float32)]
    ppermute x0 -> x46, starting transfers between devices: none -> 30.6 us  [send(): return lax.ppermute(value, 'exp', perm)]
    unnamed x12 -> x0, local copies, waits for them, and re-layouts: 16 us -> none
  transfers between devices with their start and end apart: 2 -> 46, of which waited for: 2 -> 21; matrix products, arithmetic and copies ran while one was open for 11% -> 0% of each run, Pallas kernels for 0% -> 15%
where the time goes in v1:
time: 160 us
  waiting for transfers between devices  89.7 us (56%)
  Pallas kernels  38.9 us (24%)
  starting transfers between devices  30.6 us (19%)
    ppermute x46, waiting for transfers between devices, send(): return lax.ppermute(value, 'exp', perm)  89.7 us
    ppermute x46, starting transfers between devices, send(): return lax.ppermute(value, 'exp', perm)  30.6 us
    pallas_call x7, Pallas kernels, run(): mine, other = call(spot, block, twin, *held)  24.8 us
    pallas_call x3, Pallas kernels, load(): pl.pallas_call(load_kernel, in_specs=[pl.BlockSpec(memory_space=pltpu.HBM...  9.28 us
    pallas_call x29, Pallas kernels, small(): pl.pallas_call(kernel, in_specs=[smem] + [vmem] * (len(operands) + len(ex...  3.42 us
  transfers between devices with their start and end apart: 46, of which 21 were waited for; matrix products, arithmetic and copies ran while one was open for 0% of the time, Pallas kernels for 15%

profile of v1, /device:TPU:0, one launch (start us, length us, event | category | flops | bytes accessed | tf_op | source)
XLA Modules:
  0.0 159.7 jit_solution(2587623580875110627)
XLA Ops:
  1.9 4.1 %collective-permute-start.2 = (bf16[32,3712]{1,0:T(8,128)(2,1)S(1)}, bf16[32,3712]{1,0:T(8,128)(2,1)S(1)}, u32[]{:S(2)}, u32[]{:S(2)}) collective-permute-start(bf16[32,3712]{1,0:T(8,128)(2,1)S(1)} %get-tuple-element.68), channel_id=1, source_target_pairs={{0,2},{1,3},{2,0},{3,1},{4,6},{5,7},{6,4},{7,5},{8,10},{9,11},{10,... | collective-permute-start | bytes 712712 | tf_op jit(solution)/shard_map/ppermute | solution.py:249
  7.7 5.0 %collective-permute-done.2.outer_x.inner_x = bf16[32,3712]{1,0:T(8,128)(2,1)S(1)} collective-permute-done((bf16[32,3712]{1,0:T(8,128)(2,1)S(1)}, bf16[32,3712]{1,0:T(8,128)(2,1)S(1)}, u32[]{:S(2)}, u32[]{:S(2)}) %collective-permute-start.2) | collective-permute-done | bytes 237600 | tf_op jit(solution)/shard_map/ppermute | solution.py:249
  12.7 4.0 %collective-permute-done.6.outer_y.inner_y = bf16[32,3712]{1,0:T(8,128)(2,1)S(1)} collective-permute-done((bf16[32,3712]{1,0:T(8,128)(2,1)S(1)}, bf16[32,3712]{1,0:T(8,128)(2,1)S(1)}, u32[]{:S(2)}, u32[]{:S(2)}) %collective-permute-start.6) | collective-permute-done | bytes 237600 | tf_op jit(solution)/shard_map/ppermute | solution.py:249
  26.1 3.1 %shard_map.81 = (f32[64,3584]{1,0:T(8,128)S(1)}, bf16[64,3584]{1,0:T(8,128)(2,1)S(1)}) custom-call(s32[1]{0:T(128)} %bitcast.spot, bf16[64,3712]{1,0:T(8,128)(2,1)S(1)} %shard_map.80.block, bf16[64,3712]{1,0:T(8,128)(2,1)S(1)} %collective-permute-done.8.twin, bf16[3584,1024]{1,0:T(8,128)(2,1)S(1)} %shard_map.74.gate_w, ...), custom_call_target="tpu_custom_call" | custom-call | flops 704643072 | tf_op jit(solution)/shard_map/pallas_call | solution.py:296
  32.6 6.4 %collective-permute-done.12.outer_y.inner_y = bf16[32,3712]{1,0:T(8,128)(2,1)S(1)} collective-permute-done((bf16[32,3712]{1,0:T(8,128)(2,1)S(1)}, bf16[32,3712]{1,0:T(8,128)(2,1)S(1)}, u32[]{:S(2)}, u32[]{:S(2)}) %collective-permute-start.12) | collective-permute-done | bytes 237600 | tf_op jit(solution)/shard_map/ppermute | solution.py:249
  39.0 4.2 %collective-permute-done.4.outer_x.inner_x = bf16[32,3712]{1,0:T(8,128)(2,1)S(1)} collective-permute-done((bf16[32,3712]{1,0:T(8,128)(2,1)S(1)}, bf16[32,3712]{1,0:T(8,128)(2,1)S(1)}, u32[]{:S(2)}, u32[]{:S(2)}) %collective-permute-start.4) | collective-permute-done | bytes 237600 | tf_op jit(solution)/shard_map/ppermute | solution.py:249
  51.8 6.4 %collective-permute-done.18.outer_y.refs_4_ = bf16[32,3712]{1,0:T(8,128)(2,1)S(1)} collective-permute-done((bf16[32,3712]{1,0:T(8,128)(2,1)S(1)}, bf16[32,3712]{1,0:T(8,128)(2,1)S(1)}, u32[]{:S(2)}, u32[]{:S(2)}) %collective-permute-start.18) | collective-permute-done | bytes 237600 | tf_op jit(solution)/shard_map/ppermute | solution.py:249
  58.2 4.5 %collective-permute-done.10.outer_x.refs_1_ = bf16[32,3712]{1,0:T(8,128)(2,1)S(1)} collective-permute-done((bf16[32,3712]{1,0:T(8,128)(2,1)S(1)}, bf16[32,3712]{1,0:T(8,128)(2,1)S(1)}, u32[]{:S(2)}, u32[]{:S(2)}) %collective-permute-start.10) | collective-permute-done | bytes 237600 | tf_op jit(solution)/shard_map/ppermute | solution.py:249
  64.7 3.1 %shard_map.91 = (f32[64,3584]{1,0:T(8,128)S(1)}, bf16[64,3584]{1,0:T(8,128)(2,1)S(1)}) custom-call(s32[1]{0:T(128)} %bitcast.spot, bf16[64,3712]{1,0:T(8,128)(2,1)S(1)} %shard_map.90.block, bf16[64,3712]{1,0:T(8,128)(2,1)S(1)} %collective-permute-done.20.twin, bf16[3584,1024]{1,0:T(8,128)(2,1)S(1)} %shard_map.74.gate_w, ...), custom_call_target="tpu_custom_call" | custom-call | flops 704643072 | tf_op jit(solution)/shard_map/pallas_call | solution.py:296
  68.6 3.3 %collective-permute-start.24 = (bf16[32,3712]{1,0:T(8,128)(2,1)S(1)}, bf16[32,3712]{1,0:T(8,128)(2,1)S(1)}, u32[]{:S(2)}, u32[]{:S(2)}) collective-permute-start(bf16[32,3712]{1,0:T(8,128)(2,1)S(1)} %shard_map.94), channel_id=1, source_target_pairs={{0,2},{1,3},{2,0},{3,1},{4,6},{5,7},{6,4},{7,5},{8,10},{9,11},{10,... | collective-permute-start | bytes 712712 | tf_op jit(solution)/shard_map/ppermute | solution.py:249
  72.1 6.5 %collective-permute-done.24.outer_y.other = bf16[32,3712]{1,0:T(8,128)(2,1)S(1)} collective-permute-done((bf16[32,3712]{1,0:T(8,128)(2,1)S(1)}, bf16[32,3712]{1,0:T(8,128)(2,1)S(1)}, u32[]{:S(2)}, u32[]{:S(2)}) %collective-permute-start.24) | collective-permute-done | bytes 237600 | tf_op jit(solution)/shard_map/ppermute | solution.py:249
  78.5 4.2 %collective-permute-done.16.other.outer_x = bf16[32,3712]{1,0:T(8,128)(2,1)S(1)} collective-permute-done((bf16[32,3712]{1,0:T(8,128)(2,1)S(1)}, bf16[32,3712]{1,0:T(8,128)(2,1)S(1)}, u32[]{:S(2)}, u32[]{:S(2)}) %collective-permute-start.16) | collective-permute-done | bytes 237600 | tf_op jit(solution)/shard_map/ppermute | solution.py:249
  84.9 3.2 %shard_map.97 = (f32[64,3584]{1,0:T(8,128)S(1)}, bf16[64,3584]{1,0:T(8,128)(2,1)S(1)}) custom-call(s32[1]{0:T(128)} %bitcast.spot, bf16[64,3712]{1,0:T(8,128)(2,1)S(1)} %shard_map.96.block, bf16[64,3712]{1,0:T(8,128)(2,1)S(1)} %collective-permute-done.26.twin, bf16[3584,1024]{1,0:T(8,128)(2,1)S(1)} %shard_map.74.gate_w, ...), custom_call_target="tpu_custom_call" | custom-call | flops 704643072 | tf_op jit(solution)/shard_map/pallas_call | solution.py:296
  92.1 4.9 %collective-permute-done.30.outer_y.other = bf16[32,3712]{1,0:T(8,128)(2,1)S(1)} collective-permute-done((bf16[32,3712]{1,0:T(8,128)(2,1)S(1)}, bf16[32,3712]{1,0:T(8,128)(2,1)S(1)}, u32[]{:S(2)}, u32[]{:S(2)}) %collective-permute-start.30) | collective-permute-done | bytes 237600 | tf_op jit(solution)/shard_map/ppermute | solution.py:249
  97.0 4.5 %collective-permute-done.22.other.outer_x = bf16[32,3712]{1,0:T(8,128)(2,1)S(1)} collective-permute-done((bf16[32,3712]{1,0:T(8,128)(2,1)S(1)}, bf16[32,3712]{1,0:T(8,128)(2,1)S(1)}, u32[]{:S(2)}, u32[]{:S(2)}) %collective-permute-start.22) | collective-permute-done | bytes 237600 | tf_op jit(solution)/shard_map/ppermute | solution.py:249
  103.5 3.1 %shard_map.104 = (f32[64,3584]{1,0:T(8,128)S(1)}, bf16[64,3584]{1,0:T(8,128)(2,1)S(1)}) custom-call(s32[1]{0:T(128)} %bitcast.spot, bf16[64,3712]{1,0:T(8,128)(2,1)S(1)} %shard_map.103.block, bf16[64,3712]{1,0:T(8,128)(2,1)S(1)} %collective-permute-done.32.twin, bf16[3584,1024]{1,0:T(8,128)(2,1)S(1)} %shard_map.74.gate_w, ...), custom_call_target="tpu_custom_call" | custom-call | flops 704643072 | tf_op jit(solution)/shard_map/pallas_call | solution.py:296
  110.4 6.2 %collective-permute-done.36.outer_y.other = bf16[32,3712]{1,0:T(8,128)(2,1)S(1)} collective-permute-done((bf16[32,3712]{1,0:T(8,128)(2,1)S(1)}, bf16[32,3712]{1,0:T(8,128)(2,1)S(1)}, u32[]{:S(2)}, u32[]{:S(2)}) %collective-permute-start.36) | collective-permute-done | bytes 237600 | tf_op jit(solution)/shard_map/ppermute | solution.py:249
  116.6 4.8 %collective-permute-done.28.other.outer_x = bf16[32,3712]{1,0:T(8,128)(2,1)S(1)} collective-permute-done((bf16[32,3712]{1,0:T(8,128)(2,1)S(1)}, bf16[32,3712]{1,0:T(8,128)(2,1)S(1)}, u32[]{:S(2)}, u32[]{:S(2)}) %collective-permute-start.28) | collective-permute-done | bytes 237600 | tf_op jit(solution)/shard_map/ppermute | solution.py:249
  121.8 6.0 %shard_map.77 = (f32[128,3584]{1,0:T(8,128)S(1)}, bf16[128,3584]{1,0:T(8,128)(2,1)S(1)}) custom-call(s32[1]{0:T(128)} %bitcast.spot, bf16[128,3712]{1,0:T(8,128)(2,1)S(1)} %get-tuple-element.64.after.block, bf16[128,3712]{1,0:T(8,128)(2,1)S(1)} %collective-permute-done.twin, bf16[3584,1024]{1,0:T(8,128)(2,1)S(1)} %shard_map.74.gate_w, ...), custom_call_target="tpu_custom_call" | custom-call | flops 1409286144 | tf_op jit(solution)/shard_map/pallas_call | solution.py:296
  128.5 3.1 %shard_map.111 = (f32[64,3584]{1,0:T(8,128)S(1)}, bf16[64,3584]{1,0:T(8,128)(2,1)S(1)}) custom-call(s32[1]{0:T(128)} %bitcast.spot, bf16[64,3712]{1,0:T(8,128)(2,1)S(1)} %shard_map.110.block, bf16[64,3712]{1,0:T(8,128)(2,1)S(1)} %collective-permute-done.38.twin, bf16[3584,1024]{1,0:T(8,128)(2,1)S(1)} %shard_map.74.gate_w, ...), custom_call_target="tpu_custom_call" | custom-call | flops 704643072 | tf_op jit(solution)/shard_map/pallas_call | solution.py:296
  135.0 5.9 %collective-permute-done.40.other.refs_3_ = bf16[32,3584]{1,0:T(8,128)(2,1)S(1)} collective-permute-done((bf16[32,3584]{1,0:T(8,128)(2,1)S(1)}, bf16[32,3584]{1,0:T(8,128)(2,1)S(1)}, u32[]{:S(2)}, u32[]{:S(2)}) %collective-permute-start.40) | collective-permute-done | bytes 229408 | tf_op jit(solution)/shard_map/ppermute | solution.py:249
  141.1 4.5 %collective-permute-done.34.other.refs_0_ = bf16[32,3584]{1,0:T(8,128)(2,1)S(1)} collective-permute-done((bf16[32,3584]{1,0:T(8,128)(2,1)S(1)}, bf16[32,3584]{1,0:T(8,128)(2,1)S(1)}, u32[]{:S(2)}, u32[]{:S(2)}) %collective-permute-start.34) | collective-permute-done | bytes 229408 | tf_op jit(solution)/shard_map/ppermute | solution.py:249
  148.0 6.4 %collective-permute-done.44.refs_9_.refs_10_ = bf16[32,3584]{1,0:T(8,128)(2,1)S(1)} collective-permute-done((bf16[32,3584]{1,0:T(8,128)(2,1)S(1)}, bf16[32,3584]{1,0:T(8,128)(2,1)S(1)}, u32[]{:S(2)}, u32[]{:S(2)}) %collective-permute-start.44) | collective-permute-done | bytes 229408 | tf_op jit(solution)/shard_map/ppermute | solution.py:249
  154.4 3.9 %collective-permute-done.42.refs_6_.refs_7_ = bf16[32,3584]{1,0:T(8,128)(2,1)S(1)} collective-permute-done((bf16[32,3584]{1,0:T(8,128)(2,1)S(1)}, bf16[32,3584]{1,0:T(8,128)(2,1)S(1)}, u32[]{:S(2)}, u32[]{:S(2)}) %collective-permute-start.42) | collective-permute-done | bytes 229408 | tf_op jit(solution)/shard_map/ppermute | solution.py:249
  (116 shorter events, 47.8 us)
Async XLA Ops:
  1.9 10.8 %collective-permute-start.2 = (bf16[32,3712]{1,0:T(8,128)(2,1)S(1)}, bf16[32,3712]{1,0:T(8,128)(2,1)S(1)}, u32[]{:S(2)}, u32[]{:S(2)}) collective-permute-start(bf16[32,3712]{1,0:T(8,128)(2,1)S(1)} %get-tuple-element.68), channel_id=1, source_target_pairs={{0,2},{1,3},{2,0},{3,1},{4,6},{5,7},{6,4},{7,5},{8,10},{9,11},{10,... | collective-permute-start | bytes 712712 | tf_op jit(solution)/shard_map/ppermute | solution.py:249
  6.1 10.6 %collective-permute-start.6 = (bf16[32,3712]{1,0:T(8,128)(2,1)S(1)}, bf16[32,3712]{1,0:T(8,128)(2,1)S(1)}, u32[]{:S(2)}, u32[]{:S(2)}) collective-permute-start(bf16[32,3712]{1,0:T(8,128)(2,1)S(1)} %get-tuple-element.71), channel_id=1, source_target_pairs={{0,2},{1,3},{2,0},{3,1},{4,6},{5,7},{6,4},{7,5},{8,10},{9,11},{10,... | collective-permute-start | bytes 712712 | tf_op jit(solution)/shard_map/ppermute | solution.py:249
  29.2 14.0 %collective-permute-start.9 = (bf16[64,3584]{1,0:T(8,128)(2,1)S(1)}, bf16[64,3584]{1,0:T(8,128)(2,1)S(1)}, u32[]{:S(2)}, u32[]{:S(2)}) collective-permute-start(bf16[64,3584]{1,0:T(8,128)(2,1)S(1)} %get-tuple-element.74), channel_id=1, source_target_pairs={{0,1},{1,0},{2,3},{3,2},{4,5},{5,4},{6,7},{7,6},{8,9},{9,8},{10,11... | collective-permute-start | bytes 1376264 | tf_op jit(solution)/shard_map/ppermute | solution.py:249
  32.4 10.8 %collective-permute-start.4 = (bf16[32,3712]{1,0:T(8,128)(2,1)S(1)}, bf16[32,3712]{1,0:T(8,128)(2,1)S(1)}, u32[]{:S(2)}, u32[]{:S(2)}) collective-permute-start(bf16[32,3712]{1,0:T(8,128)(2,1)S(1)} %shard_map.78), channel_id=1, source_target_pairs={{0,2},{1,3},{2,0},{3,1},{4,6},{5,7},{6,4},{7,5},{8,10},{9,11},{10,... | collective-permute-start | bytes 712712 | tf_op jit(solution)/shard_map/ppermute | solution.py:249
  32.5 10.7 %collective-permute-start.5 = (bf16[32,3712]{1,0:T(8,128)(2,1)S(1)}, bf16[32,3712]{1,0:T(8,128)(2,1)S(1)}, u32[]{:S(2)}, u32[]{:S(2)}) collective-permute-start(bf16[32,3712]{1,0:T(8,128)(2,1)S(1)} %collective-permute-done.2.outer_x.inner_x), channel_id=1, source_target_pairs={{2,4},{3,5},{4,2},{5,3},{0,1},{1,0},{6,7},{7,6},{10,12},{11,13},{1... | collective-permute-start | bytes 712712 | tf_op jit(solution)/shard_map/ppermute | solution.py:249
  48.3 14.4 %collective-permute-start.15 = (bf16[64,3584]{1,0:T(8,128)(2,1)S(1)}, bf16[64,3584]{1,0:T(8,128)(2,1)S(1)}, u32[]{:S(2)}, u32[]{:S(2)}) collective-permute-start(bf16[64,3584]{1,0:T(8,128)(2,1)S(1)} %get-tuple-element.83), channel_id=1, source_target_pairs={{0,1},{1,0},{2,3},{3,2},{4,5},{5,4},{6,7},{7,6},{8,9},{9,8},{10,11... | collective-permute-start | bytes 1376264 | tf_op jit(solution)/shard_map/ppermute | solution.py:249
  51.7 11.1 %collective-permute-start.10 = (bf16[32,3712]{1,0:T(8,128)(2,1)S(1)}, bf16[32,3712]{1,0:T(8,128)(2,1)S(1)}, u32[]{:S(2)}, u32[]{:S(2)}) collective-permute-start(bf16[32,3712]{1,0:T(8,128)(2,1)S(1)} %shard_map.82), channel_id=1, source_target_pairs={{0,2},{1,3},{2,0},{3,1},{4,6},{5,7},{6,4},{7,5},{8,10},{9,11},{10,... | collective-permute-start | bytes 712712 | tf_op jit(solution)/shard_map/ppermute | solution.py:249
  51.7 11.0 %collective-permute-start.11 = (bf16[32,3712]{1,0:T(8,128)(2,1)S(1)}, bf16[32,3712]{1,0:T(8,128)(2,1)S(1)}, u32[]{:S(2)}, u32[]{:S(2)}) collective-permute-start(bf16[32,3712]{1,0:T(8,128)(2,1)S(1)} %collective-permute-done.4.outer_x.inner_x), channel_id=1, source_target_pairs={{2,4},{3,5},{4,2},{5,3},{0,1},{1,0},{6,7},{7,6},{10,12},{11,13},{1... | collective-permute-start | bytes 712712 | tf_op jit(solution)/shard_map/ppermute | solution.py:249
  67.8 14.9 %collective-permute-start.21 = (bf16[64,3584]{1,0:T(8,128)(2,1)S(1)}, bf16[64,3584]{1,0:T(8,128)(2,1)S(1)}, u32[]{:S(2)}, u32[]{:S(2)}) collective-permute-start(bf16[64,3584]{1,0:T(8,128)(2,1)S(1)} %get-tuple-element.91), channel_id=1, source_target_pairs={{0,1},{1,0},{2,3},{3,2},{4,5},{5,4},{6,7},{7,6},{8,9},{9,8},{10,11... | collective-permute-start | bytes 1376264 | tf_op jit(solution)/shard_map/ppermute | solution.py:249
  68.0 10.5 %collective-permute-start.17 = (bf16[32,3712]{1,0:T(8,128)(2,1)S(1)}, bf16[32,3712]{1,0:T(8,128)(2,1)S(1)}, u32[]{:S(2)}, u32[]{:S(2)}) collective-permute-start(bf16[32,3712]{1,0:T(8,128)(2,1)S(1)} %get-tuple-element.67.mine.passed), channel_id=1, source_target_pairs={{2,4},{3,5},{4,2},{5,3},{0,1},{1,0},{6,7},{7,6},{10,12},{11,13},{1... | collective-permute-start | bytes 712712 | tf_op jit(solution)/shard_map/ppermute | solution.py:249
  68.6 9.9 %collective-permute-start.24 = (bf16[32,3712]{1,0:T(8,128)(2,1)S(1)}, bf16[32,3712]{1,0:T(8,128)(2,1)S(1)}, u32[]{:S(2)}, u32[]{:S(2)}) collective-permute-start(bf16[32,3712]{1,0:T(8,128)(2,1)S(1)} %shard_map.94), channel_id=1, source_target_pairs={{0,2},{1,3},{2,0},{3,1},{4,6},{5,7},{6,4},{7,5},{8,10},{9,11},{10,... | collective-permute-start | bytes 712712 | tf_op jit(solution)/shard_map/ppermute | solution.py:249
  72.0 10.8 %collective-permute-start.16 = (bf16[32,3712]{1,0:T(8,128)(2,1)S(1)}, bf16[32,3712]{1,0:T(8,128)(2,1)S(1)}, u32[]{:S(2)}, u32[]{:S(2)}) collective-permute-start(bf16[32,3712]{1,0:T(8,128)(2,1)S(1)} %shard_map.87), channel_id=1, source_target_pairs={{0,2},{1,3},{2,0},{3,1},{4,6},{5,7},{6,4},{7,5},{8,10},{9,11},{10,... | collective-permute-start | bytes 712712 | tf_op jit(solution)/shard_map/ppermute | solution.py:249
  88.0 13.5 %collective-permute-start.27 = (bf16[64,3584]{1,0:T(8,128)(2,1)S(1)}, bf16[64,3584]{1,0:T(8,128)(2,1)S(1)}, u32[]{:S(2)}, u32[]{:S(2)}) collective-permute-start(bf16[64,3584]{1,0:T(8,128)(2,1)S(1)} %get-tuple-element.99), channel_id=1, source_target_pairs={{0,1},{1,0},{2,3},{3,2},{4,5},{5,4},{6,7},{7,6},{8,9},{9,8},{10,11... | collective-permute-start | bytes 1376264 | tf_op jit(solution)/shard_map/ppermute | solution.py:249
  90.1 11.4 %collective-permute-start.22 = (bf16[32,3712]{1,0:T(8,128)(2,1)S(1)}, bf16[32,3712]{1,0:T(8,128)(2,1)S(1)}, u32[]{:S(2)}, u32[]{:S(2)}) collective-permute-start(bf16[32,3712]{1,0:T(8,128)(2,1)S(1)} %shard_map.92), channel_id=1, source_target_pairs={{0,2},{1,3},{2,0},{3,1},{4,6},{5,7},{6,4},{7,5},{8,10},{9,11},{10,... | collective-permute-start | bytes 712712 | tf_op jit(solution)/shard_map/ppermute | solution.py:249
  101.6 20.1 %collective-permute-start = (bf16[128,3712]{1,0:T(8,128)(2,1)S(1)}, bf16[128,3712]{1,0:T(8,128)(2,1)S(1)}, u32[]{:S(2)}, u32[]{:S(2)}) collective-permute-start(bf16[128,3712]{1,0:T(8,128)(2,1)S(1)} %get-tuple-element.64.after.block), channel_id=1, source_target_pairs={{0,1},{1,0},{2,3},{3,2},{4,5},{5,4},{6,7},{7,6},{8,9},{9,8},{10,11... | collective-permute-start | bytes 2850824 | tf_op jit(solution)/shard_map/ppermute | solution.py:249
  106.6 14.8 %collective-permute-start.33 = (bf16[64,3584]{1,0:T(8,128)(2,1)S(1)}, bf16[64,3584]{1,0:T(8,128)(2,1)S(1)}, u32[]{:S(2)}, u32[]{:S(2)}) collective-permute-start(bf16[64,3584]{1,0:T(8,128)(2,1)S(1)} %get-tuple-element.106), channel_id=1, source_target_pairs={{0,1},{1,0},{2,3},{3,2},{4,5},{5,4},{6,7},{7,6},{8,9},{9,8},{10,11... | collective-permute-start | bytes 1376264 | tf_op jit(solution)/shard_map/ppermute | solution.py:249
  106.9 9.7 %collective-permute-start.36 = (bf16[32,3712]{1,0:T(8,128)(2,1)S(1)}, bf16[32,3712]{1,0:T(8,128)(2,1)S(1)}, u32[]{:S(2)}, u32[]{:S(2)}) collective-permute-start(bf16[32,3712]{1,0:T(8,128)(2,1)S(1)} %shard_map.107), channel_id=1, source_target_pairs={{0,2},{1,3},{2,0},{3,1},{4,6},{5,7},{6,4},{7,5},{8,10},{9,11},{10,... | collective-permute-start | bytes 712712 | tf_op jit(solution)/shard_map/ppermute | solution.py:249
  110.1 11.3 %collective-permute-start.28 = (bf16[32,3712]{1,0:T(8,128)(2,1)S(1)}, bf16[32,3712]{1,0:T(8,128)(2,1)S(1)}, u32[]{:S(2)}, u32[]{:S(2)}) collective-permute-start(bf16[32,3712]{1,0:T(8,128)(2,1)S(1)} %shard_map.98), channel_id=1, source_target_pairs={{0,2},{1,3},{2,0},{3,1},{4,6},{5,7},{6,4},{7,5},{8,10},{9,11},{10,... | collective-permute-start | bytes 712712 | tf_op jit(solution)/shard_map/ppermute | solution.py:249
  127.8 20.2 %collective-permute-start.1 = (bf16[128,3584]{1,0:T(8,128)(2,1)S(1)}, bf16[128,3584]{1,0:T(8,128)(2,1)S(1)}, u32[]{:S(2)}, u32[]{:S(2)}) collective-permute-start(bf16[128,3584]{1,0:T(8,128)(2,1)S(1)} %get-tuple-element.66), channel_id=1, source_target_pairs={{0,1},{1,0},{2,3},{3,2},{4,5},{5,4},{6,7},{7,6},{8,9},{9,8},{10,11... | collective-permute-start | bytes 2752520 | tf_op jit(solution)/shard_map/ppermute | solution.py:249
  131.6 14.0 %collective-permute-start.39 = (bf16[64,3584]{1,0:T(8,128)(2,1)S(1)}, bf16[64,3584]{1,0:T(8,128)(2,1)S(1)}, u32[]{:S(2)}, u32[]{:S(2)}) collective-permute-start(bf16[64,3584]{1,0:T(8,128)(2,1)S(1)} %get-tuple-element.113), channel_id=1, source_target_pairs={{0,1},{1,0},{2,3},{3,2},{4,5},{5,4},{6,7},{7,6},{8,9},{9,8},{10,11... | collective-permute-start | bytes 1376264 | tf_op jit(solution)/shard_map/ppermute | solution.py:249
  134.5 11.1 %collective-permute-start.34 = (bf16[32,3584]{1,0:T(8,128)(2,1)S(1)}, bf16[32,3584]{1,0:T(8,128)(2,1)S(1)}, u32[]{:S(2)}, u32[]{:S(2)}) collective-permute-start(bf16[32,3584]{1,0:T(8,128)(2,1)S(1)} %shard_map.105), channel_id=1, source_target_pairs={{0,2},{1,3},{2,0},{3,1},{4,6},{5,7},{6,4},{7,5},{8,10},{9,11},{10,... | collective-permute-start | bytes 688136 | tf_op jit(solution)/shard_map/ppermute | solution.py:249
  134.7 10.9 %collective-permute-start.35 = (bf16[32,3584]{1,0:T(8,128)(2,1)S(1)}, bf16[32,3584]{1,0:T(8,128)(2,1)S(1)}, u32[]{:S(2)}, u32[]{:S(2)}) collective-permute-start(bf16[32,3584]{1,0:T(8,128)(2,1)S(1)} %shard_map.106), channel_id=1, source_target_pairs={{2,4},{3,5},{4,2},{5,3},{0,1},{1,0},{6,7},{7,6},{10,12},{11,13},{1... | collective-permute-start | bytes 688136 | tf_op jit(solution)/shard_map/ppermute | solution.py:249
  147.8 10.5 %collective-permute-start.42 = (bf16[32,3584]{1,0:T(8,128)(2,1)S(1)}, bf16[32,3584]{1,0:T(8,128)(2,1)S(1)}, u32[]{:S(2)}, u32[]{:S(2)}) collective-permute-start(bf16[32,3584]{1,0:T(8,128)(2,1)S(1)} %shard_map.114), channel_id=1, source_target_pairs={{0,2},{1,3},{2,0},{3,1},{4,6},{5,7},{6,4},{7,5},{8,10},{9,11},{10,... | collective-permute-start | bytes 688136 | tf_op jit(solution)/shard_map/ppermute | solution.py:249
  148.0 10.3 %collective-permute-start.43 = (bf16[32,3584]{1,0:T(8,128)(2,1)S(1)}, bf16[32,3584]{1,0:T(8,128)(2,1)S(1)}, u32[]{:S(2)}, u32[]{:S(2)}) collective-permute-start(bf16[32,3584]{1,0:T(8,128)(2,1)S(1)} %shard_map.115), channel_id=1, source_target_pairs={{2,4},{3,5},{4,2},{5,3},{0,1},{1,0},{6,7},{7,6},{10,12},{11,13},{1... | collective-permute-start | bytes 688136 | tf_op jit(solution)/shard_map/ppermute | solution.py:249
  (22 other events, 132.9 us)

commit v2 on v1

--- a/solution.py
+++ b/solution.py
@@ -97,43 +97,39 @@
     return (spot[0] < CORES) | (spot[0] >= CORES * (LINE - 1))
 
 
-def load_kernel(source, after, held, sem):
-    copy = pltpu.make_async_copy(source.at[0], held, sem)
-    copy.start()
-    copy.wait()
-
-
-def prepare_kernel(devices, placed_hbm, tokens_hbm, ids_hbm, probs_hbm, *refs):
-    outs, (placed, tokens, ids, probs, sems) = refs[:5], refs[5:]
-    rows, width = tokens.shape
-    copies = [
-        pltpu.make_async_copy(src, dst, sems.at[n])
-        for n, (src, dst) in enumerate(
-            ((placed_hbm, placed), (ids_hbm, ids), (probs_hbm, probs), (tokens_hbm, tokens))
-        )
-    ]
+def load_kernel(count, *refs):
+    sources, held, sems = refs[:count], refs[count + 1 : -1], refs[-1]
+    copies = [pltpu.make_async_copy(sources[n].at[0], held[n], sems.at[n]) for n in range(count)]
+    for copy in copies:
+        copy.start()
+    for copy in copies:
+        copy.wait()
+
+
+def prepare_kernel(devices, starts, placed_hbm, tokens_hbm, ids_hbm, probs_hbm, after, *refs):
+    outs, (placed, ids, probs, sems) = refs[: len(starts)], refs[len(starts) :]
+    count, width = ids.shape[1], tokens_hbm.shape[1]
+    moves = [(placed_hbm, placed), (ids_hbm, ids), (probs_hbm, probs)]
+    for first, out in zip(starts, outs):
+        moves.append((tokens_hbm.at[pl.ds(first, out.shape[0])], out.at[:, pl.ds(0, width)]))
+    copies = [pltpu.make_async_copy(src, dst, sems.at[n]) for n, (src, dst) in enumerate(moves)]
     for copy in copies:
         copy.start()
     for copy in copies[:3]:
         copy.wait()
-    slot = lax.broadcasted_iota(jnp.int32, (LANES, rows), 0)
-    weight = jnp.zeros((LANES, rows), jnp.float32)
+    slot = lax.broadcasted_iota(jnp.int32, (LANES, count), 0)
+    weight = jnp.zeros((LANES, count), jnp.float32)
     for s in range(devices):
-        total = jnp.zeros((1, rows), jnp.float32)
+        total = jnp.zeros((1, count), jnp.float32)
         for k in range(ids.shape[0]):
             total += jnp.where(ids[k : k + 1, :] == placed[s], probs[k : k + 1, :], 0.0)
         high = total.astype(jnp.bfloat16).astype(jnp.float32)
         weight = jnp.where(slot == s, high, jnp.where(slot == s + devices, total - high, weight))
     packed = weight.T.astype(jnp.bfloat16)
-    copies[3].wait()
-    start = 0
-    for out in outs[:-1]:
-        size = out.shape[0]
-        out[:, :width] = tokens[start : start + size, :]
-        out[:, width:] = packed[start : start + size, :]
-        start += size
-    outs[-1][:, :width] = tokens[...]
-    outs[-1][:, width:] = packed
+    for first, out in zip(starts, outs):
+        out[:, width:] = packed[first : first + out.shape[0], :]
+    for copy in copies[3:]:
+        copy.wait()
 
 
 def gate_kernel(before, out):
@@ -198,29 +194,36 @@
         out[...] = (total + other[...].astype(jnp.float32)).astype(out.dtype)
 
 
-def finish_kernel(spot, own, back, *refs):
-    out = refs[-1]
+def finish_kernel(first, start, parts, spot, own, back, *refs):
+    out, total, sem = refs[-3:]
     part, width = refs[0].shape
-    for n in range(4):
+    for n in range(parts):
         sums, near, far = refs[3 * n : 3 * n + 3]
         rows = slice(n * part, (n + 1) * part)
-        total = own[rows] + back[rows].astype(jnp.float32)
+        mine = slice(start + n * part, start + (n + 1) * part)
+        share = own[mine] + back[mine].astype(jnp.float32)
 
         @pl.when(at_end(spot))
         def _():
-            out[rows] = (total + sums[...].astype(jnp.float32)).astype(out.dtype)
+            total[rows] = (share + sums[...].astype(jnp.float32)).astype(out.dtype)
 
         @pl.when(jnp.logical_not(at_end(spot)))
         def _():
             both = near[:, :width].astype(jnp.float32) + far[...].astype(jnp.float32)
-            out[rows] = (total + both).astype(out.dtype)
+            total[rows] = (share + both).astype(out.dtype)
+
+    copy = pltpu.make_async_copy(total, out.at[pl.ds(first, parts * part)], sem)
+    copy.start()
+    copy.wait()
 
 
 def line_body(tokens, expert_ids, gate_probs, placed, w_gate, w_up, w_down):
     tok_rows, width = tokens.shape
     devices = lax.axis_size("exp")
     here = lax.axis_index("exp")
+    chip = here // CORES
     last = devices // CORES - 1
+    outer = (chip == 0) | (chip == last)
     half = tok_rows // 2
     part = half // 2
     spot = here.reshape(1).astype(jnp.int32)
@@ -250,35 +253,46 @@
 
     long = width + LANES
     given = [pltpu.with_memory_space_constraint(v, pltpu.HBM) for v in (placed, tokens, expert_ids.T, gate_probs.T)]
-    pieces = pl.pallas_call(
-        functools.partial(prepare_kernel, devices),
-        in_specs=[pl.BlockSpec(memory_space=pltpu.HBM)] * 4,
-        out_specs=[vmem] * 5,
-        out_shape=[jax.ShapeDtypeStruct((n, long), jnp.bfloat16) for n in (part,) * 4 + (tok_rows,)],
-        scratch_shapes=[pltpu.SMEM(placed.shape, placed.dtype)]
-        + [pltpu.VMEM(v.shape, v.dtype) for v in given[1:]]
-        + [pltpu.SemaphoreType.DMA((4,))],
-        compiler_params=pltpu.CompilerParams(vmem_limit_bytes=8 << 20),
-    )(*given)
-    own_a, own_b, own = pieces[:2], pieces[2:4], pieces[4]
-
-    def load(source, after):
+
+    def prepare(pieces, after):
+        starts, sizes = zip(*pieces)
         return pl.pallas_call(
-            load_kernel,
-            in_specs=[pl.BlockSpec(memory_space=pltpu.HBM), pl.BlockSpec(memory_space=pl.ANY)],
-            out_specs=vmem,
-            out_shape=pltpu.VMEM(source.shape[1:], source.dtype),
-            scratch_shapes=[pltpu.SemaphoreType.DMA],
-            cost_estimate=pl.CostEstimate(flops=source.size * 200, bytes_accessed=0, transcendentals=0),
+            functools.partial(prepare_kernel, devices, starts),
+            in_specs=[pl.BlockSpec(memory_space=pltpu.HBM)] * 4 + [pl.BlockSpec(memory_space=pl.ANY)],
+            out_specs=[vmem] * len(pieces),
+            out_shape=[jax.ShapeDtypeStruct((size, long), jnp.bfloat16) for size in sizes],
+            scratch_shapes=[pltpu.SMEM(placed.shape, placed.dtype)]
+            + [pltpu.VMEM(v.shape, v.dtype) for v in given[2:]]
+            + [pltpu.SemaphoreType.DMA((3 + len(pieces),))],
+            compiler_params=pltpu.CompilerParams(vmem_limit_bytes=4 << 20),
+        )(*given, after)
+
+    own_a = prepare([(0, part), (part, part)], given[0])
+    own_b = prepare([(half, part), (half + part, part), (0, half), (half, half)], own_a[0])
+    own_b, own_whole = own_b[:2], own_b[2:]
+
+    hbm = pl.BlockSpec(memory_space=pltpu.HBM)
+
+    def load(sources, after):
+        count = len(sources)
+        return pl.pallas_call(
+            functools.partial(load_kernel, count),
+            in_specs=[hbm] * count + [pl.BlockSpec(memory_space=pl.ANY)],
+            out_specs=[vmem] * count,
+            out_shape=[pltpu.VMEM(w.shape[1:], w.dtype) for w in sources],
+            scratch_shapes=[pltpu.SemaphoreType.DMA((count,))],
+            cost_estimate=pl.CostEstimate(
+                flops=count * sources[0].size * 200, bytes_accessed=0, transcendentals=0
+            ),
             compiler_params=pltpu.CompilerParams(vmem_limit_bytes=1 << 20),
-        )(pltpu.with_memory_space_constraint(source, pltpu.HBM), after)
-
-    held = [load(w, own) for w in (w_gate, w_up, w_down)]
-
-    def run(block, twin=None):
+        )(*[pltpu.with_memory_space_constraint(w, pltpu.HBM) for w in sources], after)
+
+    held = load((w_gate, w_up), own_a[0])
+    held += load((w_down,), own_a[0])
+
+    def run(block):
         count = block.shape[0]
-        if twin is None:
-            twin = send(block, twins)
+        twin = send(block, twins)
         call = pl.pallas_call(
             functools.partial(run_kernel, width, devices),
             in_specs=[smem] + [vmem] * 5,
@@ -334,8 +348,8 @@
         m[slot][n] = send(middle_rows, middle)
 
     def after(slot, n, result):
-        g[slot][n], m[slot][n], result = lax.optimization_barrier((g[slot][n], m[slot][n], result))
-        return result
+        g[slot][n], m[slot][n], mine = lax.optimization_barrier((g[slot][n], m[slot][n], result[:1]))
+        return mine + result[1:]
 
     def block(outer_rows, inner_rows):
         return small(join_kernel, (half, long), *outer_rows, *inner_rows, extra=(gates[-1],))
@@ -354,48 +368,53 @@
 
     start(0, 0)
     start(0, 1)
+    here_a = run(own_whole[0])
     after(0, 0, ())
     start(1, 0)
     gate()
-    after(0, 1, ())
     start(1, 1)
     near_a = after(1, 0, run(block(g[0], g[0])))
     start(2, 0)
     gate()
-    after(1, 1, ())
     start(2, 1)
     mid_a = after(2, 0, run(block(g[1], m[0])))
     start(3, 0)
     gate()
-    after(2, 1, ())
     start(3, 1)
     far_a = after(3, 0, run(block(g[2], m[1])))
     start(4, 0)
     gate()
-    after(3, 1, ())
     start(4, 1)
     far_b = after(4, 0, run(block(g[3], m[2])))
     start(5, 0)
     gate()
-    after(4, 1, ())
     start(5, 1)
     mid_b = after(5, 0, run(block(g[4], m[3])))
     start(6, 0)
     gate()
-    after(5, 1, ())
     start(6, 1)
     near_b = after(6, 0, run(block(g[5], g[1])))
     start(7, 0)
     gate()
-    after(6, 1, ())
     start(7, 1)
-    mine, back = run(own)
-    ends = []
-    for n in range(2):
-        ends += [g[6][n], g[2][n], m[4][n]]
-    for n in range(2):
-        ends += [g[7][n], g[7][n], m[7][n]]
-    return small(finish_kernel, (tok_rows, width), mine, back, *ends, extra=(gates[-1],))
+    here_b = run(own_whole[1])
+
+    def finish(first, sums, ends, *extra):
+        operands = (*sums, *(v for triple in ends for v in triple))
+        parts = len(ends)
+        return pl.pallas_call(
+            functools.partial(finish_kernel, first, first % half, parts),
+            in_specs=[smem] + [vmem] * len(operands) + [pl.BlockSpec(memory_space=pl.ANY)] * len(extra),
+            out_specs=hbm,
+            out_shape=jax.ShapeDtypeStruct((tok_rows, width), jnp.bfloat16),
+            scratch_shapes=[pltpu.VMEM((parts * part, width), jnp.bfloat16), pltpu.SemaphoreType.DMA],
+            input_output_aliases={len(operands) + 1: 0} if first else {},
+            compiler_params=pltpu.CompilerParams(vmem_limit_bytes=8 << 20),
+        )(spot, *operands, *extra)
+
+    rows = finish(0, here_a, [(g[6][n], g[2][n], m[4][n]) for n in range(2)], gates[-1])
+    rows = finish(half, here_b, [(g[7][0], g[7][0], m[7][0])], rows)
+    return finish(half + part, here_b, [(g[7][1], g[7][1], m[7][1])], rows)
 
 
 def body(tokens, *rest):

time: 160 us -> 135 us (0.84)
  waiting for transfers between devices: 89.7 us -> 29.9 us
  starting transfers between devices: 30.6 us -> 62.3 us
  Pallas kernels: 38.9 us -> 40.7 us
    ppermute x46 -> x48, waiting for transfers between devices: 89.7 us -> 29.9 us  [send(): return lax.ppermute(value, 'exp', perm)]
    ppermute x46 -> x48, starting transfers between devices: 30.6 us -> 62.3 us  [send(): return lax.ppermute(value, 'exp', perm)]
    pallas_call x4 -> x7, Pallas kernels: 10.7 us -> 13.5 us  [the longest x2 8.28 us: load(): pl.pallas_call(functools.partial(load_kernel, count), in_specs=[hbm] * co...]
    pallas_call x29 -> x28, Pallas kernels: 3.42 us -> 1.89 us  [small(): pl.pallas_call(kernel, in_specs=[smem] + [vmem] * (len(operands) + len(ex...]
    pallas_call x7 -> x8, Pallas kernels: 24.8 us -> 25.3 us  [run(): mine, other = call(spot, block, twin, *held)]
  transfers between devices with their start and end apart: 46 -> 48, of which waited for: 21 -> 11; matrix products, arithmetic and copies ran while one was open for 0% -> 0% of each run, Pallas kernels for 15% -> 29%
where the time goes in v2:
time: 135 us; the launch traced here: 134 us
  starting transfers between devices  62.3 us (46%)
  Pallas kernels  40.7 us (30%)
  waiting for transfers between devices  29.9 us (22%)
    ppermute x48, starting transfers between devices, send(): return lax.ppermute(value, 'exp', perm)  62.3 us
    ppermute x48, waiting for transfers between devices, send(): return lax.ppermute(value, 'exp', perm)  29.9 us
    pallas_call x8, Pallas kernels, run(): mine, other = call(spot, block, twin, *held)  25.3 us
    pallas_call x2, Pallas kernels, load(): pl.pallas_call(functools.partial(load_kernel, count), in_specs=[hbm] * co...  8.28 us
  transfers between devices with their start and end apart: 48, of which 11 were waited for; matrix products, arithmetic and copies ran while one was open for 0% of the time, Pallas kernels for 29%

profile of v2, /device:TPU:0, one launch (start us, length us, event | category | flops | bytes accessed | tf_op | source)
XLA Modules:
  0.0 133.7 jit_solution(9465629877030258828)
XLA Ops:
  1.1 3.1 %collective-permute-start.2 = (bf16[32,3712]{1,0:T(8,128)(2,1)S(1)}, bf16[32,3712]{1,0:T(8,128)(2,1)S(1)}, u32[]{:S(2)}, u32[]{:S(2)}) collective-permute-start(bf16[32,3712]{1,0:T(8,128)(2,1)S(1)} %get-tuple-element.49.after.refs_2_.refs_1_), channel_id=1, source_target_pairs={{0,2},{1,3},{2,0},{3,1},{4,6},{5,7},{6,4},{7,5},{8,10},{9,11},{10,... | collective-permute-start | bytes 712712 | tf_op jit(solution)/shard_map/ppermute | solution.py:252
  4.3 3.1 %collective-permute-start.6 = (bf16[32,3712]{1,0:T(8,128)(2,1)S(1)}, bf16[32,3712]{1,0:T(8,128)(2,1)S(1)}, u32[]{:S(2)}, u32[]{:S(2)}) collective-permute-start(bf16[32,3712]{1,0:T(8,128)(2,1)S(1)} %get-tuple-element.58), channel_id=1, source_target_pairs={{0,2},{1,3},{2,0},{3,1},{4,6},{5,7},{6,4},{7,5},{8,10},{9,11},{10,... | collective-permute-start | bytes 712712 | tf_op jit(solution)/shard_map/ppermute | solution.py:252
  7.4 3.5 %collective-permute-done.2.outer_x.inner_x = bf16[32,3712]{1,0:T(8,128)(2,1)S(1)} collective-permute-done((bf16[32,3712]{1,0:T(8,128)(2,1)S(1)}, bf16[32,3712]{1,0:T(8,128)(2,1)S(1)}, u32[]{:S(2)}, u32[]{:S(2)}) %collective-permute-start.2) | collective-permute-done | bytes 237600 | tf_op jit(solution)/shard_map/ppermute | solution.py:252
  10.9 4.2 %collective-permute-done.6.outer_y.inner_y = bf16[32,3712]{1,0:T(8,128)(2,1)S(1)} collective-permute-done((bf16[32,3712]{1,0:T(8,128)(2,1)S(1)}, bf16[32,3712]{1,0:T(8,128)(2,1)S(1)}, u32[]{:S(2)}, u32[]{:S(2)}) %collective-permute-start.6) | collective-permute-done | bytes 237600 | tf_op jit(solution)/shard_map/ppermute | solution.py:252
  17.4 3.3 %collective-permute-start.4 = (bf16[32,3712]{1,0:T(8,128)(2,1)S(1)}, bf16[32,3712]{1,0:T(8,128)(2,1)S(1)}, u32[]{:S(2)}, u32[]{:S(2)}) collective-permute-start(bf16[32,3712]{1,0:T(8,128)(2,1)S(1)} %shard_map.78), channel_id=1, source_target_pairs={{0,2},{1,3},{2,0},{3,1},{4,6},{5,7},{6,4},{7,5},{8,10},{9,11},{10,... | collective-permute-start | bytes 712712 | tf_op jit(solution)/shard_map/ppermute | solution.py:252
  20.7 5.0 %collective-permute-start.12 = (bf16[32,3712]{1,0:T(8,128)(2,1)S(1)}, bf16[32,3712]{1,0:T(8,128)(2,1)S(1)}, u32[]{:S(2)}, u32[]{:S(2)}) collective-permute-start(bf16[32,3712]{1,0:T(8,128)(2,1)S(1)} %shard_map.83), channel_id=1, source_target_pairs={{0,2},{1,3},{2,0},{3,1},{4,6},{5,7},{6,4},{7,5},{8,10},{9,11},{10,... | collective-permute-start | bytes 712712 | tf_op jit(solution)/shard_map/ppermute | solution.py:252
  25.8 3.1 %shard_map.76.down_w = bf16[1024,3584]{1,0:T(8,128)(2,1)S(1)} custom-call(bf16[1,1024,3584]{2,1,0:T(8,128)(2,1)} %refs_0_.3, bf16[32,3712]{1,0:T(8,128)(2,1)S(1)} %get-tuple-element.49.after.refs_2_.refs_1_), custom_call_target="tpu_custom_call" | custom-call | flops 734003200 | tf_op jit(solution)/shard_map/pallas_call | solution.py:278
  28.9 5.2 %shard_map.75 = (bf16[3584,1024]{1,0:T(8,128)(2,1)S(1)}, bf16[3584,1024]{1,0:T(8,128)(2,1)S(1)}) custom-call(bf16[1,3584,1024]{2,1,0:T(8,128)(2,1)} %refs_0_.2, bf16[1,3584,1024]{2,1,0:T(8,128)(2,1)} %refs_1_.1, bf16[32,3712]{1,0:T(8,128)(2,1)S(1)} %get-tuple-element.49.after.refs_2_.refs_1_), custom_call_target="tpu_custom_call" | custom-call | flops 1468006400 | tf_op jit(solution)/shard_map/pallas_call | solution.py:278
  34.1 3.2 %shard_map.81 = (f32[64,3584]{1,0:T(8,128)S(1)}, bf16[64,3584]{1,0:T(8,128)(2,1)S(1)}) custom-call(s32[1]{0:T(128)} %bitcast.spot, bf16[64,3712]{1,0:T(8,128)(2,1)S(1)} %shard_map.80.block, bf16[64,3712]{1,0:T(8,128)(2,1)S(1)} %collective-permute-done.7.twin, bf16[3584,1024]{1,0:T(8,128)(2,1)S(1)} %get-tuple-element.51.gate_w, ...), custom_call_target="tpu_custom_call" | custom-call | flops 704643072 | tf_op jit(solution)/shard_map/pallas_call | solution.py:310
  40.2 6.5 %collective-permute-start.18 = (bf16[32,3712]{1,0:T(8,128)(2,1)S(1)}, bf16[32,3712]{1,0:T(8,128)(2,1)S(1)}, u32[]{:S(2)}, u32[]{:S(2)}) collective-permute-start(bf16[32,3712]{1,0:T(8,128)(2,1)S(1)} %shard_map.88), channel_id=1, source_target_pairs={{0,2},{1,3},{2,0},{3,1},{4,6},{5,7},{6,4},{7,5},{8,10},{9,11},{10,... | collective-permute-start | bytes 712712 | tf_op jit(solution)/shard_map/ppermute | solution.py:252
  46.8 3.2 %shard_map.86 = (f32[64,3584]{1,0:T(8,128)S(1)}, bf16[64,3584]{1,0:T(8,128)(2,1)S(1)}) custom-call(s32[1]{0:T(128)} %bitcast.spot, bf16[64,3712]{1,0:T(8,128)(2,1)S(1)} %shard_map.85.block, bf16[64,3712]{1,0:T(8,128)(2,1)S(1)} %collective-permute-done.13.twin, bf16[3584,1024]{1,0:T(8,128)(2,1)S(1)} %get-tuple-element.51.gate_w, ...), custom_call_target="tpu_custom_call" | custom-call | flops 704643072 | tf_op jit(solution)/shard_map/pallas_call | solution.py:310
  55.2 6.6 %collective-permute-start.24 = (bf16[32,3712]{1,0:T(8,128)(2,1)S(1)}, bf16[32,3712]{1,0:T(8,128)(2,1)S(1)}, u32[]{:S(2)}, u32[]{:S(2)}) collective-permute-start(bf16[32,3712]{1,0:T(8,128)(2,1)S(1)} %shard_map.94), channel_id=1, source_target_pairs={{0,2},{1,3},{2,0},{3,1},{4,6},{5,7},{6,4},{7,5},{8,10},{9,11},{10,... | collective-permute-start | bytes 712712 | tf_op jit(solution)/shard_map/ppermute | solution.py:252
  61.8 3.2 %shard_map.91 = (f32[64,3584]{1,0:T(8,128)S(1)}, bf16[64,3584]{1,0:T(8,128)(2,1)S(1)}) custom-call(s32[1]{0:T(128)} %bitcast.spot, bf16[64,3712]{1,0:T(8,128)(2,1)S(1)} %shard_map.90.block, bf16[64,3712]{1,0:T(8,128)(2,1)S(1)} %collective-permute-done.19.twin, bf16[3584,1024]{1,0:T(8,128)(2,1)S(1)} %get-tuple-element.51.gate_w, ...), custom_call_target="tpu_custom_call" | custom-call | flops 704643072 | tf_op jit(solution)/shard_map/pallas_call | solution.py:310
  70.6 6.3 %collective-permute-start.30 = (bf16[32,3712]{1,0:T(8,128)(2,1)S(1)}, bf16[32,3712]{1,0:T(8,128)(2,1)S(1)}, u32[]{:S(2)}, u32[]{:S(2)}) collective-permute-start(bf16[32,3712]{1,0:T(8,128)(2,1)S(1)} %shard_map.100), channel_id=1, source_target_pairs={{0,2},{1,3},{2,0},{3,1},{4,6},{5,7},{6,4},{7,5},{8,10},{9,11},{10,... | collective-permute-start | bytes 712712 | tf_op jit(solution)/shard_map/ppermute | solution.py:252
  77.0 3.2 %shard_map.97 = (f32[64,3584]{1,0:T(8,128)S(1)}, bf16[64,3584]{1,0:T(8,128)(2,1)S(1)}) custom-call(s32[1]{0:T(128)} %bitcast.spot, bf16[64,3712]{1,0:T(8,128)(2,1)S(1)} %shard_map.96.block, bf16[64,3712]{1,0:T(8,128)(2,1)S(1)} %collective-permute-done.25.twin, bf16[3584,1024]{1,0:T(8,128)(2,1)S(1)} %get-tuple-element.51.gate_w, ...), custom_call_target="tpu_custom_call" | custom-call | flops 704643072 | tf_op jit(solution)/shard_map/pallas_call | solution.py:310
  85.4 3.2 %shard_map.103 = (f32[64,3584]{1,0:T(8,128)S(1)}, bf16[64,3584]{1,0:T(8,128)(2,1)S(1)}) custom-call(s32[1]{0:T(128)} %bitcast.spot, bf16[64,3712]{1,0:T(8,128)(2,1)S(1)} %shard_map.102.block, bf16[64,3712]{1,0:T(8,128)(2,1)S(1)} %collective-permute-done.31.twin, bf16[3584,1024]{1,0:T(8,128)(2,1)S(1)} %get-tuple-element.51.gate_w, ...), custom_call_target="tpu_custom_call" | custom-call | flops 704643072 | tf_op jit(solution)/shard_map/pallas_call | solution.py:310
  91.3 4.6 %collective-permute-done.35.outer_y.other = bf16[32,3712]{1,0:T(8,128)(2,1)S(1)} collective-permute-done((bf16[32,3712]{1,0:T(8,128)(2,1)S(1)}, bf16[32,3712]{1,0:T(8,128)(2,1)S(1)}, u32[]{:S(2)}, u32[]{:S(2)}) %collective-permute-start.35) | collective-permute-done | bytes 237600 | tf_op jit(solution)/shard_map/ppermute | solution.py:252
  97.4 3.2 %shard_map.117 = (f32[64,3584]{1,0:T(8,128)S(1)}, bf16[64,3584]{1,0:T(8,128)(2,1)S(1)}) custom-call(s32[1]{0:T(128)} %bitcast.spot, bf16[64,3712]{1,0:T(8,128)(2,1)S(1)} %get-tuple-element.89.block, bf16[64,3712]{1,0:T(8,128)(2,1)S(1)} %collective-permute-done.45.twin, bf16[3584,1024]{1,0:T(8,128)(2,1)S(1)} %get-tuple-element.51.gate_w, ...), custom_call_target="tpu_custom_call" | custom-call | flops 704643072 | tf_op jit(solution)/shard_map/pallas_call | solution.py:310
  100.8 3.2 %shard_map.109 = (f32[64,3584]{1,0:T(8,128)S(1)}, bf16[64,3584]{1,0:T(8,128)(2,1)S(1)}) custom-call(s32[1]{0:T(128)} %bitcast.spot, bf16[64,3712]{1,0:T(8,128)(2,1)S(1)} %shard_map.108.block, bf16[64,3712]{1,0:T(8,128)(2,1)S(1)} %collective-permute-done.36.twin, bf16[3584,1024]{1,0:T(8,128)(2,1)S(1)} %get-tuple-element.51.gate_w, ...), custom_call_target="tpu_custom_call" | custom-call | flops 704643072 | tf_op jit(solution)/shard_map/pallas_call | solution.py:310
  104.7 3.7 %collective-permute-start.41 = (bf16[32,3584]{1,0:T(8,128)(2,1)S(1)}, bf16[32,3584]{1,0:T(8,128)(2,1)S(1)}, u32[]{:S(2)}, u32[]{:S(2)}) collective-permute-start(bf16[32,3584]{1,0:T(8,128)(2,1)S(1)} %shard_map.113), channel_id=1, source_target_pairs={{0,2},{1,3},{2,0},{3,1},{4,6},{5,7},{6,4},{7,5},{8,10},{9,11},{10,... | collective-permute-start | bytes 688136 | tf_op jit(solution)/shard_map/ppermute | solution.py:252
  108.5 3.2 %shard_map.77 = (f32[64,3584]{1,0:T(8,128)S(1)}, bf16[64,3584]{1,0:T(8,128)(2,1)S(1)}) custom-call(s32[1]{0:T(128)} %bitcast.spot, bf16[64,3712]{1,0:T(8,128)(2,1)S(1)} %get-tuple-element.50.block, bf16[64,3712]{1,0:T(8,128)(2,1)S(1)} %collective-permute-done.twin, bf16[3584,1024]{1,0:T(8,128)(2,1)S(1)} %get-tuple-element.51.gate_w, ...), custom_call_target="tpu_custom_call" | custom-call | flops 704643072 | tf_op jit(solution)/shard_map/pallas_call | solution.py:310
  114.9 3.6 %collective-permute-done.33.other.refs_0_ = bf16[32,3584]{1,0:T(8,128)(2,1)S(1)} collective-permute-done((bf16[32,3584]{1,0:T(8,128)(2,1)S(1)}, bf16[32,3584]{1,0:T(8,128)(2,1)S(1)}, u32[]{:S(2)}, u32[]{:S(2)}) %collective-permute-start.33) | collective-permute-done | bytes 229408 | tf_op jit(solution)/shard_map/ppermute | solution.py:252
  119.3 3.4 %collective-permute-start.43 = (bf16[32,3584]{1,0:T(8,128)(2,1)S(1)}, bf16[32,3584]{1,0:T(8,128)(2,1)S(1)}, u32[]{:S(2)}, u32[]{:S(2)}) collective-permute-start(bf16[32,3584]{1,0:T(8,128)(2,1)S(1)} %shard_map.115), channel_id=1, source_target_pairs={{0,2},{1,3},{2,0},{3,1},{4,6},{5,7},{6,4},{7,5},{8,10},{9,11},{10,... | collective-permute-start | bytes 688136 | tf_op jit(solution)/shard_map/ppermute | solution.py:252
  122.8 5.9 %collective-permute-start.39 = (bf16[32,3584]{1,0:T(8,128)(2,1)S(1)}, bf16[32,3584]{1,0:T(8,128)(2,1)S(1)}, u32[]{:S(2)}, u32[]{:S(2)}) collective-permute-start(bf16[32,3584]{1,0:T(8,128)(2,1)S(1)} %shard_map.111), channel_id=1, source_target_pairs={{0,2},{1,3},{2,0},{3,1},{4,6},{5,7},{6,4},{7,5},{8,10},{9,11},{10,... | collective-permute-start | bytes 688136 | tf_op jit(solution)/shard_map/ppermute | solution.py:252
  (123 shorter events, 36.5 us)
Async XLA Ops:
  4.3 10.9 %collective-permute-start.6 = (bf16[32,3712]{1,0:T(8,128)(2,1)S(1)}, bf16[32,3712]{1,0:T(8,128)(2,1)S(1)}, u32[]{:S(2)}, u32[]{:S(2)}) collective-permute-start(bf16[32,3712]{1,0:T(8,128)(2,1)S(1)} %get-tuple-element.58), channel_id=1, source_target_pairs={{0,2},{1,3},{2,0},{3,1},{4,6},{5,7},{6,4},{7,5},{8,10},{9,11},{10,... | collective-permute-start | bytes 712712 | tf_op jit(solution)/shard_map/ppermute | solution.py:252
  15.2 18.9 %collective-permute-start.7 = (bf16[64,3712]{1,0:T(8,128)(2,1)S(1)}, bf16[64,3712]{1,0:T(8,128)(2,1)S(1)}, u32[]{:S(2)}, u32[]{:S(2)}) collective-permute-start(bf16[64,3712]{1,0:T(8,128)(2,1)S(1)} %shard_map.80.block), channel_id=1, source_target_pairs={{0,1},{1,0},{2,3},{3,2},{4,5},{5,4},{6,7},{7,6},{8,9},{9,8},{10,11... | collective-permute-start | bytes 1425416 | tf_op jit(solution)/shard_map/ppermute | solution.py:252
  17.2 20.1 %collective-permute-start.5 = (bf16[32,3712]{1,0:T(8,128)(2,1)S(1)}, bf16[32,3712]{1,0:T(8,128)(2,1)S(1)}, u32[]{:S(2)}, u32[]{:S(2)}) collective-permute-start(bf16[32,3712]{1,0:T(8,128)(2,1)S(1)} %collective-permute-done.2.outer_x.inner_x), channel_id=1, source_target_pairs={{2,4},{3,5},{4,2},{5,3},{0,1},{1,0},{6,7},{7,6},{10,12},{11,13},{1... | collective-permute-start | bytes 712712 | tf_op jit(solution)/shard_map/ppermute | solution.py:252
  17.4 20.0 %collective-permute-start.4 = (bf16[32,3712]{1,0:T(8,128)(2,1)S(1)}, bf16[32,3712]{1,0:T(8,128)(2,1)S(1)}, u32[]{:S(2)}, u32[]{:S(2)}) collective-permute-start(bf16[32,3712]{1,0:T(8,128)(2,1)S(1)} %shard_map.78), channel_id=1, source_target_pairs={{0,2},{1,3},{2,0},{3,1},{4,6},{5,7},{6,4},{7,5},{8,10},{9,11},{10,... | collective-permute-start | bytes 712712 | tf_op jit(solution)/shard_map/ppermute | solution.py:252
  20.7 16.6 %collective-permute-start.12 = (bf16[32,3712]{1,0:T(8,128)(2,1)S(1)}, bf16[32,3712]{1,0:T(8,128)(2,1)S(1)}, u32[]{:S(2)}, u32[]{:S(2)}) collective-permute-start(bf16[32,3712]{1,0:T(8,128)(2,1)S(1)} %shard_map.83), channel_id=1, source_target_pairs={{0,2},{1,3},{2,0},{3,1},{4,6},{5,7},{6,4},{7,5},{8,10},{9,11},{10,... | collective-permute-start | bytes 712712 | tf_op jit(solution)/shard_map/ppermute | solution.py:252
  38.1 11.9 %collective-permute-start.10 = (bf16[32,3712]{1,0:T(8,128)(2,1)S(1)}, bf16[32,3712]{1,0:T(8,128)(2,1)S(1)}, u32[]{:S(2)}, u32[]{:S(2)}) collective-permute-start(bf16[32,3712]{1,0:T(8,128)(2,1)S(1)} %collective-permute-done.4.outer_x.inner_x), channel_id=1, source_target_pairs={{2,4},{3,5},{4,2},{5,3},{0,1},{1,0},{6,7},{7,6},{10,12},{11,13},{1... | collective-permute-start | bytes 712712 | tf_op jit(solution)/shard_map/ppermute | solution.py:252
  39.2 10.8 %collective-permute-start.9 = (bf16[32,3712]{1,0:T(8,128)(2,1)S(1)}, bf16[32,3712]{1,0:T(8,128)(2,1)S(1)}, u32[]{:S(2)}, u32[]{:S(2)}) collective-permute-start(bf16[32,3712]{1,0:T(8,128)(2,1)S(1)} %shard_map.82), channel_id=1, source_target_pairs={{0,2},{1,3},{2,0},{3,1},{4,6},{5,7},{6,4},{7,5},{8,10},{9,11},{10,... | collective-permute-start | bytes 712712 | tf_op jit(solution)/shard_map/ppermute | solution.py:252
  40.2 12.0 %collective-permute-start.18 = (bf16[32,3712]{1,0:T(8,128)(2,1)S(1)}, bf16[32,3712]{1,0:T(8,128)(2,1)S(1)}, u32[]{:S(2)}, u32[]{:S(2)}) collective-permute-start(bf16[32,3712]{1,0:T(8,128)(2,1)S(1)} %shard_map.88), channel_id=1, source_target_pairs={{0,2},{1,3},{2,0},{3,1},{4,6},{5,7},{6,4},{7,5},{8,10},{9,11},{10,... | collective-permute-start | bytes 712712 | tf_op jit(solution)/shard_map/ppermute | solution.py:252
  52.8 12.2 %collective-permute-start.16 = (bf16[32,3712]{1,0:T(8,128)(2,1)S(1)}, bf16[32,3712]{1,0:T(8,128)(2,1)S(1)}, u32[]{:S(2)}, u32[]{:S(2)}) collective-permute-start(bf16[32,3712]{1,0:T(8,128)(2,1)S(1)} %get-tuple-element.55.mine.passed), channel_id=1, source_target_pairs={{2,4},{3,5},{4,2},{5,3},{0,1},{1,0},{6,7},{7,6},{10,12},{11,13},{1... | collective-permute-start | bytes 712712 | tf_op jit(solution)/shard_map/ppermute | solution.py:252
  52.9 12.1 %collective-permute-start.15 = (bf16[32,3712]{1,0:T(8,128)(2,1)S(1)}, bf16[32,3712]{1,0:T(8,128)(2,1)S(1)}, u32[]{:S(2)}, u32[]{:S(2)}) collective-permute-start(bf16[32,3712]{1,0:T(8,128)(2,1)S(1)} %shard_map.87), channel_id=1, source_target_pairs={{0,2},{1,3},{2,0},{3,1},{4,6},{5,7},{6,4},{7,5},{8,10},{9,11},{10,... | collective-permute-start | bytes 712712 | tf_op jit(solution)/shard_map/ppermute | solution.py:252
  55.2 11.5 %collective-permute-start.24 = (bf16[32,3712]{1,0:T(8,128)(2,1)S(1)}, bf16[32,3712]{1,0:T(8,128)(2,1)S(1)}, u32[]{:S(2)}, u32[]{:S(2)}) collective-permute-start(bf16[32,3712]{1,0:T(8,128)(2,1)S(1)} %shard_map.94), channel_id=1, source_target_pairs={{0,2},{1,3},{2,0},{3,1},{4,6},{5,7},{6,4},{7,5},{8,10},{9,11},{10,... | collective-permute-start | bytes 712712 | tf_op jit(solution)/shard_map/ppermute | solution.py:252
  66.8 10.2 %collective-permute-start.25 = (bf16[64,3712]{1,0:T(8,128)(2,1)S(1)}, bf16[64,3712]{1,0:T(8,128)(2,1)S(1)}, u32[]{:S(2)}, u32[]{:S(2)}) collective-permute-start(bf16[64,3712]{1,0:T(8,128)(2,1)S(1)} %shard_map.96.block), channel_id=1, source_target_pairs={{0,1},{1,0},{2,3},{3,2},{4,5},{5,4},{6,7},{7,6},{8,9},{9,8},{10,11... | collective-permute-start | bytes 1425416 | tf_op jit(solution)/shard_map/ppermute | solution.py:252
  67.6 13.1 %collective-permute-start.21 = (bf16[32,3712]{1,0:T(8,128)(2,1)S(1)}, bf16[32,3712]{1,0:T(8,128)(2,1)S(1)}, u32[]{:S(2)}, u32[]{:S(2)}) collective-permute-start(bf16[32,3712]{1,0:T(8,128)(2,1)S(1)} %shard_map.92), channel_id=1, source_target_pairs={{0,2},{1,3},{2,0},{3,1},{4,6},{5,7},{6,4},{7,5},{8,10},{9,11},{10,... | collective-permute-start | bytes 712712 | tf_op jit(solution)/shard_map/ppermute | solution.py:252
  70.6 11.8 %collective-permute-start.30 = (bf16[32,3712]{1,0:T(8,128)(2,1)S(1)}, bf16[32,3712]{1,0:T(8,128)(2,1)S(1)}, u32[]{:S(2)}, u32[]{:S(2)}) collective-permute-start(bf16[32,3712]{1,0:T(8,128)(2,1)S(1)} %shard_map.100), channel_id=1, source_target_pairs={{0,2},{1,3},{2,0},{3,1},{4,6},{5,7},{6,4},{7,5},{8,10},{9,11},{10,... | collective-permute-start | bytes 712712 | tf_op jit(solution)/shard_map/ppermute | solution.py:252
  84.4 11.5 %collective-permute-start.35 = (bf16[32,3712]{1,0:T(8,128)(2,1)S(1)}, bf16[32,3712]{1,0:T(8,128)(2,1)S(1)}, u32[]{:S(2)}, u32[]{:S(2)}) collective-permute-start(bf16[32,3712]{1,0:T(8,128)(2,1)S(1)} %shard_map.106), channel_id=1, source_target_pairs={{0,2},{1,3},{2,0},{3,1},{4,6},{5,7},{6,4},{7,5},{8,10},{9,11},{10,... | collective-permute-start | bytes 712712 | tf_op jit(solution)/shard_map/ppermute | solution.py:252
  84.9 12.5 %collective-permute-start.45 = (bf16[64,3712]{1,0:T(8,128)(2,1)S(1)}, bf16[64,3712]{1,0:T(8,128)(2,1)S(1)}, u32[]{:S(2)}, u32[]{:S(2)}) collective-permute-start(bf16[64,3712]{1,0:T(8,128)(2,1)S(1)} %get-tuple-element.89.block), channel_id=1, source_target_pairs={{0,1},{1,0},{2,3},{3,2},{4,5},{5,4},{6,7},{7,6},{8,9},{9,8},{10,11... | collective-permute-start | bytes 1425416 | tf_op jit(solution)/shard_map/ppermute | solution.py:252
  96.3 12.1 %collective-permute-start = (bf16[64,3712]{1,0:T(8,128)(2,1)S(1)}, bf16[64,3712]{1,0:T(8,128)(2,1)S(1)}, u32[]{:S(2)}, u32[]{:S(2)}) collective-permute-start(bf16[64,3712]{1,0:T(8,128)(2,1)S(1)} %get-tuple-element.50.block), channel_id=1, source_target_pairs={{0,1},{1,0},{2,3},{3,2},{4,5},{5,4},{6,7},{7,6},{8,9},{9,8},{10,11... | collective-permute-start | bytes 1425416 | tf_op jit(solution)/shard_map/ppermute | solution.py:252
  100.6 22.1 %collective-permute-start.46 = (bf16[64,3584]{1,0:T(8,128)(2,1)S(1)}, bf16[64,3584]{1,0:T(8,128)(2,1)S(1)}, u32[]{:S(2)}, u32[]{:S(2)}) collective-permute-start(bf16[64,3584]{1,0:T(8,128)(2,1)S(1)} %get-tuple-element.91), channel_id=1, source_target_pairs={{0,1},{1,0},{2,3},{3,2},{4,5},{5,4},{6,7},{7,6},{8,9},{9,8},{10,11... | collective-permute-start | bytes 1376264 | tf_op jit(solution)/shard_map/ppermute | solution.py:252
  104.0 14.7 %collective-permute-start.37 = (bf16[64,3584]{1,0:T(8,128)(2,1)S(1)}, bf16[64,3584]{1,0:T(8,128)(2,1)S(1)}, u32[]{:S(2)}, u32[]{:S(2)}) collective-permute-start(bf16[64,3584]{1,0:T(8,128)(2,1)S(1)} %get-tuple-element.86), channel_id=1, source_target_pairs={{0,1},{1,0},{2,3},{3,2},{4,5},{5,4},{6,7},{7,6},{8,9},{9,8},{10,11... | collective-permute-start | bytes 1376264 | tf_op jit(solution)/shard_map/ppermute | solution.py:252
  104.7 10.2 %collective-permute-start.41 = (bf16[32,3584]{1,0:T(8,128)(2,1)S(1)}, bf16[32,3584]{1,0:T(8,128)(2,1)S(1)}, u32[]{:S(2)}, u32[]{:S(2)}) collective-permute-start(bf16[32,3584]{1,0:T(8,128)(2,1)S(1)} %shard_map.113), channel_id=1, source_target_pairs={{0,2},{1,3},{2,0},{3,1},{4,6},{5,7},{6,4},{7,5},{8,10},{9,11},{10,... | collective-permute-start | bytes 688136 | tf_op jit(solution)/shard_map/ppermute | solution.py:252
  108.4 10.1 %collective-permute-start.33 = (bf16[32,3584]{1,0:T(8,128)(2,1)S(1)}, bf16[32,3584]{1,0:T(8,128)(2,1)S(1)}, u32[]{:S(2)}, u32[]{:S(2)}) collective-permute-start(bf16[32,3584]{1,0:T(8,128)(2,1)S(1)} %shard_map.104), channel_id=1, source_target_pairs={{0,2},{1,3},{2,0},{3,1},{4,6},{5,7},{6,4},{7,5},{8,10},{9,11},{10,... | collective-permute-start | bytes 688136 | tf_op jit(solution)/shard_map/ppermute | solution.py:252
  114.8 14.9 %collective-permute-start.1 = (bf16[64,3584]{1,0:T(8,128)(2,1)S(1)}, bf16[64,3584]{1,0:T(8,128)(2,1)S(1)}, u32[]{:S(2)}, u32[]{:S(2)}) collective-permute-start(bf16[64,3584]{1,0:T(8,128)(2,1)S(1)} %get-tuple-element.54), channel_id=1, source_target_pairs={{0,1},{1,0},{2,3},{3,2},{4,5},{5,4},{6,7},{7,6},{8,9},{9,8},{10,11... | collective-permute-start | bytes 1376264 | tf_op jit(solution)/shard_map/ppermute | solution.py:252
  118.7 11.0 %collective-permute-start.44 = (bf16[32,3584]{1,0:T(8,128)(2,1)S(1)}, bf16[32,3584]{1,0:T(8,128)(2,1)S(1)}, u32[]{:S(2)}, u32[]{:S(2)}) collective-permute-start(bf16[32,3584]{1,0:T(8,128)(2,1)S(1)} %shard_map.116), channel_id=1, source_target_pairs={{2,4},{3,5},{4,2},{5,3},{0,1},{1,0},{6,7},{7,6},{10,12},{11,13},{1... | collective-permute-start | bytes 688136 | tf_op jit(solution)/shard_map/ppermute | solution.py:252
  119.3 10.4 %collective-permute-start.43 = (bf16[32,3584]{1,0:T(8,128)(2,1)S(1)}, bf16[32,3584]{1,0:T(8,128)(2,1)S(1)}, u32[]{:S(2)}, u32[]{:S(2)}) collective-permute-start(bf16[32,3584]{1,0:T(8,128)(2,1)S(1)} %shard_map.115), channel_id=1, source_target_pairs={{0,2},{1,3},{2,0},{3,1},{4,6},{5,7},{6,4},{7,5},{8,10},{9,11},{10,... | collective-permute-start | bytes 688136 | tf_op jit(solution)/shard_map/ppermute | solution.py:252
  (24 other events, 135.2 us)

commit v3 on v2

--- a/solution.py
+++ b/solution.py
@@ -76,11 +76,15 @@
     return mixed.astype(jnp.bfloat16)
 
 
-def run_kernel(width, devices, spot, block, twin, gate_w, up_w, down_w, own, other, rows):
+def run_kernel(width, devices, spot, block, twin, gate_w, up_w, down_w, own, other_x, other_y, rows):
     half = own.shape[0]
     rows[:half] = block[...]
     rows[half:] = twin[...]
     lane = lax.broadcasted_iota(jnp.int32, (2 * half, LANES), 1)
+    row = lax.broadcasted_iota(jnp.int32, (2 * half, LANES), 0)
+    part = half // 2
+    lower = ((row >= part) & (row < half)) | (row >= half + part)
+    lane = jnp.where(lower, lane - 2 * devices, lane)
     mine = (lane == spot[0]) | (lane == spot[0] + devices)
     weights = rows[:, width:].astype(jnp.float32)
     scale = jnp.sum(jnp.where(mine, weights, 0.0), axis=1, keepdims=True)
@@ -90,7 +94,8 @@
     hidden = (gate / (1.0 + jnp.exp(-gate)) * up).astype(jnp.bfloat16)
     result = jnp.dot(hidden, down_w[...], preferred_element_type=jnp.float32) * scale
     own[...] = result[:half]
-    other[...] = result[half:].astype(jnp.bfloat16)
+    other_x[...] = result[half : half + part].astype(jnp.bfloat16)
+    other_y[...] = result[half + part :].astype(jnp.bfloat16)
 
 
 def at_end(spot):
@@ -106,7 +111,7 @@
         copy.wait()
 
 
-def prepare_kernel(devices, starts, placed_hbm, tokens_hbm, ids_hbm, probs_hbm, after, *refs):
+def prepare_kernel(devices, part, starts, placed_hbm, tokens_hbm, ids_hbm, probs_hbm, after, *refs):
     outs, (placed, ids, probs, sems) = refs[: len(starts)], refs[len(starts) :]
     count, width = ids.shape[1], tokens_hbm.shape[1]
     moves = [(placed_hbm, placed), (ids_hbm, ids), (probs_hbm, probs)]
@@ -124,10 +129,17 @@
         for k in range(ids.shape[0]):
             total += jnp.where(ids[k : k + 1, :] == placed[s], probs[k : k + 1, :], 0.0)
         high = total.astype(jnp.bfloat16).astype(jnp.float32)
-        weight = jnp.where(slot == s, high, jnp.where(slot == s + devices, total - high, weight))
+        for base in (s, s + 2 * devices):
+            weight = jnp.where(slot == base, high, jnp.where(slot == base + devices, total - high, weight))
     packed = weight.T.astype(jnp.bfloat16)
+    lane = lax.broadcasted_iota(jnp.int32, (part, LANES), 1)
     for first, out in zip(starts, outs):
-        out[:, width:] = packed[first : first + out.shape[0], :]
+        if out.shape[1] > width:
+            upper = packed[first : first + part, :]
+            lower = packed[first + part : first + 2 * part, :]
+            both = jnp.where(lane < 2 * devices, upper.astype(jnp.float32), lower.astype(jnp.float32))
+            for row in range(0, out.shape[0], part):
+                out[row : row + part, width:] = both.astype(jnp.bfloat16)
     for copy in copies[3:]:
         copy.wait()
 
@@ -137,17 +149,20 @@
 
 
 def join_kernel(spot, outer_x, outer_y, inner_x, inner_y, gate, out):
-    part = outer_x.shape[0]
+    part, width = outer_y.shape
+
+    def put(upper, lower):
+        out[:part] = upper[...]
+        out[part:, :width] = lower[...]
+        out[part:, width:] = upper[:, width:]
 
     @pl.when(at_end(spot))
     def _():
-        out[:part] = outer_x[...]
-        out[part:] = outer_y[...]
+        put(outer_x, outer_y)
 
     @pl.when(jnp.logical_not(at_end(spot)))
     def _():
-        out[:part] = inner_x[...]
-        out[part:] = inner_y[...]
+        put(inner_x, inner_y)
 
 
 def over_kernel(start, spot, own, back, passed, out):
@@ -155,9 +170,10 @@
 
     @pl.when(at_end(spot))
     def _():
-        total = own[start : start + part] + back[start : start + part].astype(jnp.float32)
+        total = own[start : start + part] + back[...].astype(jnp.float32)
         out[:, :width] = total.astype(out.dtype)
-        out[:, width:] = jnp.zeros((part, out.shape[1] - width), out.dtype)
+        if out.shape[1] > width:
+            out[:, width:] = jnp.zeros((part, out.shape[1] - width), out.dtype)
 
     @pl.when(jnp.logical_not(at_end(spot)))
     def _():
@@ -176,7 +192,7 @@
 
 def add_kernel(start, spot, own, back, other, out):
     part, width = out.shape
-    total = own[start : start + part] + back[start : start + part].astype(jnp.float32)
+    total = own[start : start + part] + back[...].astype(jnp.float32)
     out[...] = (total + other[:, :width].astype(jnp.float32)).astype(out.dtype)
 
 
@@ -185,23 +201,23 @@
 
     @pl.when(at_end(spot))
     def _():
-        total = outer_own[start : start + part] + outer_back[start : start + part].astype(jnp.float32)
+        total = outer_own[start : start + part] + outer_back[...].astype(jnp.float32)
         out[...] = total.astype(out.dtype)
 
     @pl.when(jnp.logical_not(at_end(spot)))
     def _():
-        total = inner_own[start : start + part] + inner_back[start : start + part].astype(jnp.float32)
+        total = inner_own[start : start + part] + inner_back[...].astype(jnp.float32)
         out[...] = (total + other[...].astype(jnp.float32)).astype(out.dtype)
 
 
-def finish_kernel(first, start, parts, spot, own, back, *refs):
-    out, total, sem = refs[-3:]
+def finish_kernel(first, start, parts, spot, own, *refs):
+    backs, refs, (out, total, sem) = refs[:parts], refs[parts:-3], refs[-3:]
     part, width = refs[0].shape
     for n in range(parts):
         sums, near, far = refs[3 * n : 3 * n + 3]
         rows = slice(n * part, (n + 1) * part)
         mine = slice(start + n * part, start + (n + 1) * part)
-        share = own[mine] + back[mine].astype(jnp.float32)
+        share = own[mine] + backs[n][...].astype(jnp.float32)
 
         @pl.when(at_end(spot))
         def _():
@@ -221,9 +237,7 @@
     tok_rows, width = tokens.shape
     devices = lax.axis_size("exp")
     here = lax.axis_index("exp")
-    chip = here // CORES
     last = devices // CORES - 1
-    outer = (chip == 0) | (chip == last)
     half = tok_rows // 2
     part = half // 2
     spot = here.reshape(1).astype(jnp.int32)
@@ -255,20 +269,21 @@
     given = [pltpu.with_memory_space_constraint(v, pltpu.HBM) for v in (placed, tokens, expert_ids.T, gate_probs.T)]
 
     def prepare(pieces, after):
-        starts, sizes = zip(*pieces)
+        starts = [first for first, _, _ in pieces]
         return pl.pallas_call(
-            functools.partial(prepare_kernel, devices, starts),
+            functools.partial(prepare_kernel, devices, part, starts),
             in_specs=[pl.BlockSpec(memory_space=pltpu.HBM)] * 4 + [pl.BlockSpec(memory_space=pl.ANY)],
             out_specs=[vmem] * len(pieces),
-            out_shape=[jax.ShapeDtypeStruct((size, long), jnp.bfloat16) for size in sizes],
+            out_shape=[jax.ShapeDtypeStruct(shape, jnp.bfloat16) for _, *shape in pieces],
             scratch_shapes=[pltpu.SMEM(placed.shape, placed.dtype)]
             + [pltpu.VMEM(v.shape, v.dtype) for v in given[2:]]
             + [pltpu.SemaphoreType.DMA((3 + len(pieces),))],
             compiler_params=pltpu.CompilerParams(vmem_limit_bytes=4 << 20),
         )(*given, after)
 
-    own_a = prepare([(0, part), (part, part)], given[0])
-    own_b = prepare([(half, part), (half + part, part), (0, half), (half, half)], own_a[0])
+    own_a = prepare([(0, part, long), (part, part, width)], given[0])
+    others = [(half, part, long), (half + part, part, width), (0, half, long), (half, half, long)]
+    own_b = prepare(others, own_a[0])
     own_b, own_whole = own_b[:2], own_b[2:]
 
     hbm = pl.BlockSpec(memory_space=pltpu.HBM)
@@ -296,19 +311,17 @@
         call = pl.pallas_call(
             functools.partial(run_kernel, width, devices),
             in_specs=[smem] + [vmem] * 5,
-            out_specs=[vmem, vmem],
-            out_shape=[
-                jax.ShapeDtypeStruct((count, width), jnp.float32),
-                jax.ShapeDtypeStruct((count, width), jnp.bfloat16),
-            ],
+            out_specs=[vmem] * 3,
+            out_shape=[jax.ShapeDtypeStruct((count, width), jnp.float32)]
+            + [jax.ShapeDtypeStruct((part, width), jnp.bfloat16)] * 2,
             scratch_shapes=[pltpu.VMEM((2 * count, long), jnp.bfloat16)],
             cost_estimate=pl.CostEstimate(
                 flops=count * width * w_gate.shape[2] * 3, bytes_accessed=0, transcendentals=0
             ),
             compiler_params=pltpu.CompilerParams(vmem_limit_bytes=count * (160 << 10)),
         )
-        mine, other = call(spot, block, twin, *held)
-        return mine, send(other, twins)
+        mine, other_x, other_y = call(spot, block, twin, *held)
+        return mine, send(other_x, twins), send(other_y, twins)
 
     g = [[None, None] for _ in range(8)]
     m = [[None, None] for _ in range(8)]
@@ -318,19 +331,20 @@
         first = n * part
 
         def over(sums, passed):
-            return small(functools.partial(over_kernel, first), (part, long), *sums, passed)
+            return small(functools.partial(over_kernel, first), passed.shape, sums[0], sums[1 + n], passed)
 
         def between(sums, other):
-            return small(functools.partial(add_kernel, first), (part, width), *sums, other)
+            return small(functools.partial(add_kernel, first), (part, width), sums[0], sums[1 + n], other)
 
         def ends(outer_sums, inner_sums, other):
             kernel = functools.partial(ends_kernel, first)
-            return small(kernel, (part, width), *outer_sums, *inner_sums, other)
+            sums = (outer_sums[0], outer_sums[1 + n], inner_sums[0], inner_sums[1 + n])
+            return small(kernel, (part, width), *sums, other)
 
         if slot == 0:
             pair_rows, middle_rows = own_a[n], own_a[n]
         elif slot == 1:
-            pair_rows = small(pass_kernel, (part, long), own_b[n], m[0][n])
+            pair_rows = small(pass_kernel, own_b[n].shape, own_b[n], m[0][n])
             middle_rows = g[0][n]
         elif slot == 2:
             pair_rows, middle_rows = over(near_a, m[1][n]), g[1][n]
@@ -413,8 +427,8 @@
         )(spot, *operands, *extra)
 
     rows = finish(0, here_a, [(g[6][n], g[2][n], m[4][n]) for n in range(2)], gates[-1])
-    rows = finish(half, here_b, [(g[7][0], g[7][0], m[7][0])], rows)
-    return finish(half + part, here_b, [(g[7][1], g[7][1], m[7][1])], rows)
+    rows = finish(half, here_b[:2], [(g[7][0], g[7][0], m[7][0])], rows)
+    return finish(half + part, here_b[::2], [(g[7][1], g[7][1], m[7][1])], rows)
 
 
 def body(tokens, *rest):

time: 135 us -> 141 us (1.044)
  starting transfers between devices: 62.3 us -> 67.3 us
    ppermute x48 -> x56, starting transfers between devices: 62.3 us -> 67.3 us  [send(): return lax.ppermute(value, 'exp', perm)]
    ppermute x48 -> x56, waiting for transfers between devices: 29.9 us -> 30.1 us  [send(): return lax.ppermute(value, 'exp', perm)]
  transfers between devices with their start and end apart: 48 -> 56, of which waited for: 11 -> 16; matrix products, arithmetic and copies ran while one was open for 0% -> 0% of each run, Pallas kernels for 29% -> 28%
where the time goes in v3:
time: 141 us; the launch traced here: 139 us
  starting transfers between devices  67.3 us (48%)
  Pallas kernels  41.1 us (29%)
  waiting for transfers between devices  30.1 us (21%)
    ppermute x56, starting transfers between devices, send(): return lax.ppermute(value, 'exp', perm)  67.3 us
    ppermute x56, waiting for transfers between devices, send(): return lax.ppermute(value, 'exp', perm)  30.1 us
    pallas_call x8, Pallas kernels, run(): mine, other_x, other_y = call(spot, block, twin, *held)  25.5 us
    pallas_call x2, Pallas kernels, load(): pl.pallas_call(functools.partial(load_kernel, count), in_specs=[hbm] * co...  8.28 us
  transfers between devices with their start and end apart: 56, of which 16 were waited for; matrix products, arithmetic and copies ran while one was open for 0% of the time, Pallas kernels for 28%

profile of v3, /device:TPU:0, one launch (start us, length us, event | category | flops | bytes accessed | tf_op | source)
XLA Modules:
  0.0 139.2 jit_solution(9418975222740349859)
XLA Ops:
  1.1 3.1 %collective-permute-start.2 = (bf16[32,3712]{1,0:T(8,128)(2,1)S(1)}, bf16[32,3712]{1,0:T(8,128)(2,1)S(1)}, u32[]{:S(2)}, u32[]{:S(2)}) collective-permute-start(bf16[32,3712]{1,0:T(8,128)(2,1)S(1)} %get-tuple-element.57.after.refs_2_.refs_1_), channel_id=1, source_target_pairs={{0,2},{1,3},{2,0},{3,1},{4,6},{5,7},{6,4},{7,5},{8,10},{9,11},{10,... | collective-permute-start | bytes 712712 | tf_op jit(solution)/shard_map/ppermute | solution.py:266
  4.3 3.1 %collective-permute-start.6 = (bf16[32,3584]{1,0:T(8,128)(2,1)S(1)}, bf16[32,3584]{1,0:T(8,128)(2,1)S(1)}, u32[]{:S(2)}, u32[]{:S(2)}) collective-permute-start(bf16[32,3584]{1,0:T(8,128)(2,1)S(1)} %get-tuple-element.66), channel_id=1, source_target_pairs={{0,2},{1,3},{2,0},{3,1},{4,6},{5,7},{6,4},{7,5},{8,10},{9,11},{10,... | collective-permute-start | bytes 688136 | tf_op jit(solution)/shard_map/ppermute | solution.py:266
  7.4 3.5 %collective-permute-done.2.outer_x.inner_x = bf16[32,3712]{1,0:T(8,128)(2,1)S(1)} collective-permute-done((bf16[32,3712]{1,0:T(8,128)(2,1)S(1)}, bf16[32,3712]{1,0:T(8,128)(2,1)S(1)}, u32[]{:S(2)}, u32[]{:S(2)}) %collective-permute-start.2) | collective-permute-done | bytes 237600 | tf_op jit(solution)/shard_map/ppermute | solution.py:266
  10.9 4.1 %collective-permute-done.6.outer_y.inner_y = bf16[32,3584]{1,0:T(8,128)(2,1)S(1)} collective-permute-done((bf16[32,3584]{1,0:T(8,128)(2,1)S(1)}, bf16[32,3584]{1,0:T(8,128)(2,1)S(1)}, u32[]{:S(2)}, u32[]{:S(2)}) %collective-permute-start.6) | collective-permute-done | bytes 229408 | tf_op jit(solution)/shard_map/ppermute | solution.py:266
  17.3 7.6 %collective-permute-start.12 = (bf16[32,3584]{1,0:T(8,128)(2,1)S(1)}, bf16[32,3584]{1,0:T(8,128)(2,1)S(1)}, u32[]{:S(2)}, u32[]{:S(2)}) collective-permute-start(bf16[32,3584]{1,0:T(8,128)(2,1)S(1)} %shard_map.83), channel_id=1, source_target_pairs={{0,2},{1,3},{2,0},{3,1},{4,6},{5,7},{6,4},{7,5},{8,10},{9,11},{10,... | collective-permute-start | bytes 688136 | tf_op jit(solution)/shard_map/ppermute | solution.py:266
  26.6 3.1 %shard_map.76.down_w = bf16[1024,3584]{1,0:T(8,128)(2,1)S(1)} custom-call(bf16[1,1024,3584]{2,1,0:T(8,128)(2,1)} %refs_0_.3, bf16[32,3712]{1,0:T(8,128)(2,1)S(1)} %get-tuple-element.57.after.refs_2_.refs_1_), custom_call_target="tpu_custom_call" | custom-call | flops 734003200 | tf_op jit(solution)/shard_map/pallas_call | solution.py:293
  29.7 5.2 %shard_map.75 = (bf16[3584,1024]{1,0:T(8,128)(2,1)S(1)}, bf16[3584,1024]{1,0:T(8,128)(2,1)S(1)}) custom-call(bf16[1,3584,1024]{2,1,0:T(8,128)(2,1)} %refs_0_.2, bf16[1,3584,1024]{2,1,0:T(8,128)(2,1)} %refs_1_.1, bf16[32,3712]{1,0:T(8,128)(2,1)S(1)} %get-tuple-element.57.after.refs_2_.refs_1_), custom_call_target="tpu_custom_call" | custom-call | flops 1468006400 | tf_op jit(solution)/shard_map/pallas_call | solution.py:293
  35.0 3.2 %shard_map.81 = (f32[64,3584]{1,0:T(8,128)S(1)}, bf16[32,3584]{1,0:T(8,128)(2,1)S(1)}, bf16[32,3584]{1,0:T(8,128)(2,1)S(1)}) custom-call(s32[1]{0:T(128)} %bitcast.spot, bf16[64,3712]{1,0:T(8,128)(2,1)S(1)} %shard_map.80.block, bf16[64,3712]{1,0:T(8,128)(2,1)S(1)} %collective-permute-done.7.twin, bf16[3584,1024]{1,0:T(8,128)(2,1)S(1)} %get-tuple-element.59.gate_w, ...), custom_call_target="tpu_custom_call" | custom-call | flops 704643072 | tf_op jit(solution)/shard_map/pallas_call | solution.py:323
  41.4 6.4 %collective-permute-start.19 = (bf16[32,3584]{1,0:T(8,128)(2,1)S(1)}, bf16[32,3584]{1,0:T(8,128)(2,1)S(1)}, u32[]{:S(2)}, u32[]{:S(2)}) collective-permute-start(bf16[32,3584]{1,0:T(8,128)(2,1)S(1)} %shard_map.88), channel_id=1, source_target_pairs={{0,2},{1,3},{2,0},{3,1},{4,6},{5,7},{6,4},{7,5},{8,10},{9,11},{10,... | collective-permute-start | bytes 688136 | tf_op jit(solution)/shard_map/ppermute | solution.py:266
  47.8 3.2 %shard_map.86 = (f32[64,3584]{1,0:T(8,128)S(1)}, bf16[32,3584]{1,0:T(8,128)(2,1)S(1)}, bf16[32,3584]{1,0:T(8,128)(2,1)S(1)}) custom-call(s32[1]{0:T(128)} %bitcast.spot, bf16[64,3712]{1,0:T(8,128)(2,1)S(1)} %shard_map.85.block, bf16[64,3712]{1,0:T(8,128)(2,1)S(1)} %collective-permute-done.13.twin, bf16[3584,1024]{1,0:T(8,128)(2,1)S(1)} %get-tuple-element.59.gate_w, ...), custom_call_target="tpu_custom_call" | custom-call | flops 704643072 | tf_op jit(solution)/shard_map/pallas_call | solution.py:323
  51.0 2.4 %collective-permute-done.19.outer_y.refs_6_ = bf16[32,3584]{1,0:T(8,128)(2,1)S(1)} collective-permute-done((bf16[32,3584]{1,0:T(8,128)(2,1)S(1)}, bf16[32,3584]{1,0:T(8,128)(2,1)S(1)}, u32[]{:S(2)}, u32[]{:S(2)}) %collective-permute-start.19) | collective-permute-done | bytes 229408 | tf_op jit(solution)/shard_map/ppermute | solution.py:266
  57.0 6.4 %collective-permute-start.26 = (bf16[32,3584]{1,0:T(8,128)(2,1)S(1)}, bf16[32,3584]{1,0:T(8,128)(2,1)S(1)}, u32[]{:S(2)}, u32[]{:S(2)}) collective-permute-start(bf16[32,3584]{1,0:T(8,128)(2,1)S(1)} %shard_map.94), channel_id=1, source_target_pairs={{0,2},{1,3},{2,0},{3,1},{4,6},{5,7},{6,4},{7,5},{8,10},{9,11},{10,... | collective-permute-start | bytes 688136 | tf_op jit(solution)/shard_map/ppermute | solution.py:266
  63.3 3.2 %shard_map.91 = (f32[64,3584]{1,0:T(8,128)S(1)}, bf16[32,3584]{1,0:T(8,128)(2,1)S(1)}, bf16[32,3584]{1,0:T(8,128)(2,1)S(1)}) custom-call(s32[1]{0:T(128)} %bitcast.spot, bf16[64,3712]{1,0:T(8,128)(2,1)S(1)} %shard_map.90.block, bf16[64,3712]{1,0:T(8,128)(2,1)S(1)} %collective-permute-done.20.twin, bf16[3584,1024]{1,0:T(8,128)(2,1)S(1)} %get-tuple-element.59.gate_w, ...), custom_call_target="tpu_custom_call" | custom-call | flops 704643072 | tf_op jit(solution)/shard_map/pallas_call | solution.py:323
  72.6 6.4 %collective-permute-start.33 = (bf16[32,3584]{1,0:T(8,128)(2,1)S(1)}, bf16[32,3584]{1,0:T(8,128)(2,1)S(1)}, u32[]{:S(2)}, u32[]{:S(2)}) collective-permute-start(bf16[32,3584]{1,0:T(8,128)(2,1)S(1)} %shard_map.100), channel_id=1, source_target_pairs={{0,2},{1,3},{2,0},{3,1},{4,6},{5,7},{6,4},{7,5},{8,10},{9,11},{10,... | collective-permute-start | bytes 688136 | tf_op jit(solution)/shard_map/ppermute | solution.py:266
  79.1 3.2 %shard_map.97 = (f32[64,3584]{1,0:T(8,128)S(1)}, bf16[32,3584]{1,0:T(8,128)(2,1)S(1)}, bf16[32,3584]{1,0:T(8,128)(2,1)S(1)}) custom-call(s32[1]{0:T(128)} %bitcast.spot, bf16[64,3712]{1,0:T(8,128)(2,1)S(1)} %shard_map.96.block, bf16[64,3712]{1,0:T(8,128)(2,1)S(1)} %collective-permute-done.27.twin, bf16[3584,1024]{1,0:T(8,128)(2,1)S(1)} %get-tuple-element.59.gate_w, ...), custom_call_target="tpu_custom_call" | custom-call | flops 704643072 | tf_op jit(solution)/shard_map/pallas_call | solution.py:323
  89.6 3.2 %shard_map.103 = (f32[64,3584]{1,0:T(8,128)S(1)}, bf16[32,3584]{1,0:T(8,128)(2,1)S(1)}, bf16[32,3584]{1,0:T(8,128)(2,1)S(1)}) custom-call(s32[1]{0:T(128)} %bitcast.spot, bf16[64,3712]{1,0:T(8,128)(2,1)S(1)} %shard_map.102.block, bf16[64,3712]{1,0:T(8,128)(2,1)S(1)} %collective-permute-done.34.twin, bf16[3584,1024]{1,0:T(8,128)(2,1)S(1)} %get-tuple-element.59.gate_w, ...), custom_call_target="tpu_custom_call" | custom-call | flops 704643072 | tf_op jit(solution)/shard_map/pallas_call | solution.py:323
  94.9 4.1 %collective-permute-done.39.outer_y.other = bf16[32,3584]{1,0:T(8,128)(2,1)S(1)} collective-permute-done((bf16[32,3584]{1,0:T(8,128)(2,1)S(1)}, bf16[32,3584]{1,0:T(8,128)(2,1)S(1)}, u32[]{:S(2)}, u32[]{:S(2)}) %collective-permute-start.39) | collective-permute-done | bytes 229408 | tf_op jit(solution)/shard_map/ppermute | solution.py:266
  103.9 8.0 %collective-permute-start.46 = (bf16[32,3584]{1,0:T(8,128)(2,1)S(1)}, bf16[32,3584]{1,0:T(8,128)(2,1)S(1)}, u32[]{:S(2)}, u32[]{:S(2)}) collective-permute-start(bf16[32,3584]{1,0:T(8,128)(2,1)S(1)} %shard_map.113), channel_id=1, source_target_pairs={{0,2},{1,3},{2,0},{3,1},{4,6},{5,7},{6,4},{7,5},{8,10},{9,11},{10,... | collective-permute-start | bytes 688136 | tf_op jit(solution)/shard_map/ppermute | solution.py:266
  111.9 3.2 %shard_map.109 = (f32[64,3584]{1,0:T(8,128)S(1)}, bf16[32,3584]{1,0:T(8,128)(2,1)S(1)}, bf16[32,3584]{1,0:T(8,128)(2,1)S(1)}) custom-call(s32[1]{0:T(128)} %bitcast.spot, bf16[64,3712]{1,0:T(8,128)(2,1)S(1)} %shard_map.108.block, bf16[64,3712]{1,0:T(8,128)(2,1)S(1)} %collective-permute-done.40.twin, bf16[3584,1024]{1,0:T(8,128)(2,1)S(1)} %get-tuple-element.59.gate_w, ...), custom_call_target="tpu_custom_call" | custom-call | flops 704643072 | tf_op jit(solution)/shard_map/pallas_call | solution.py:323
  115.3 3.2 %shard_map.117 = (f32[64,3584]{1,0:T(8,128)S(1)}, bf16[32,3584]{1,0:T(8,128)(2,1)S(1)}, bf16[32,3584]{1,0:T(8,128)(2,1)S(1)}) custom-call(s32[1]{0:T(128)} %bitcast.spot, bf16[64,3712]{1,0:T(8,128)(2,1)S(1)} %get-tuple-element.104.block, bf16[64,3712]{1,0:T(8,128)(2,1)S(1)} %collective-permute-done.52.twin, bf16[3584,1024]{1,0:T(8,128)(2,1)S(1)} %get-tuple-element.59.gate_w, ...), custom_call_target="tpu_custom_call" | custom-call | flops 704643072 | tf_op jit(solution)/shard_map/pallas_call | solution.py:323
  118.5 3.2 %shard_map.77 = (f32[64,3584]{1,0:T(8,128)S(1)}, bf16[32,3584]{1,0:T(8,128)(2,1)S(1)}, bf16[32,3584]{1,0:T(8,128)(2,1)S(1)}) custom-call(s32[1]{0:T(128)} %bitcast.spot, bf16[64,3712]{1,0:T(8,128)(2,1)S(1)} %get-tuple-element.58.block, bf16[64,3712]{1,0:T(8,128)(2,1)S(1)} %collective-permute-done.twin, bf16[3584,1024]{1,0:T(8,128)(2,1)S(1)} %get-tuple-element.59.gate_w, ...), custom_call_target="tpu_custom_call" | custom-call | flops 704643072 | tf_op jit(solution)/shard_map/pallas_call | solution.py:323
  123.9 3.6 %collective-permute-start.50 = (bf16[32,3584]{1,0:T(8,128)(2,1)S(1)}, bf16[32,3584]{1,0:T(8,128)(2,1)S(1)}, u32[]{:S(2)}, u32[]{:S(2)}) collective-permute-start(bf16[32,3584]{1,0:T(8,128)(2,1)S(1)} %shard_map.115), channel_id=1, source_target_pairs={{0,2},{1,3},{2,0},{3,1},{4,6},{5,7},{6,4},{7,5},{8,10},{9,11},{10,... | collective-permute-start | bytes 688136 | tf_op jit(solution)/shard_map/ppermute | solution.py:266
  128.0 5.4 %collective-permute-start.43 = (bf16[32,3584]{1,0:T(8,128)(2,1)S(1)}, bf16[32,3584]{1,0:T(8,128)(2,1)S(1)}, u32[]{:S(2)}, u32[]{:S(2)}) collective-permute-start(bf16[32,3584]{1,0:T(8,128)(2,1)S(1)} %shard_map.111), channel_id=1, source_target_pairs={{0,2},{1,3},{2,0},{3,1},{4,6},{5,7},{6,4},{7,5},{8,10},{9,11},{10,... | collective-permute-start | bytes 688136 | tf_op jit(solution)/shard_map/ppermute | solution.py:266
  135.3 2.9 %collective-permute-done.43.refs_1_.refs_2_ = bf16[32,3584]{1,0:T(8,128)(2,1)S(1)} collective-permute-done((bf16[32,3584]{1,0:T(8,128)(2,1)S(1)}, bf16[32,3584]{1,0:T(8,128)(2,1)S(1)}, u32[]{:S(2)}, u32[]{:S(2)}) %collective-permute-start.43) | collective-permute-done | bytes 229408 | tf_op jit(solution)/shard_map/ppermute | solution.py:266
  (139 shorter events, 37.6 us)
Async XLA Ops:
  4.3 10.7 %collective-permute-start.6 = (bf16[32,3584]{1,0:T(8,128)(2,1)S(1)}, bf16[32,3584]{1,0:T(8,128)(2,1)S(1)}, u32[]{:S(2)}, u32[]{:S(2)}) collective-permute-start(bf16[32,3584]{1,0:T(8,128)(2,1)S(1)} %get-tuple-element.66), channel_id=1, source_target_pairs={{0,2},{1,3},{2,0},{3,1},{4,6},{5,7},{6,4},{7,5},{8,10},{9,11},{10,... | collective-permute-start | bytes 688136 | tf_op jit(solution)/shard_map/ppermute | solution.py:266
  15.0 20.0 %collective-permute-start.7 = (bf16[64,3712]{1,0:T(8,128)(2,1)S(1)}, bf16[64,3712]{1,0:T(8,128)(2,1)S(1)}, u32[]{:S(2)}, u32[]{:S(2)}) collective-permute-start(bf16[64,3712]{1,0:T(8,128)(2,1)S(1)} %shard_map.80.block), channel_id=1, source_target_pairs={{0,1},{1,0},{2,3},{3,2},{4,5},{5,4},{6,7},{7,6},{8,9},{9,8},{10,11... | collective-permute-start | bytes 1425416 | tf_op jit(solution)/shard_map/ppermute | solution.py:266
  17.3 20.9 %collective-permute-start.12 = (bf16[32,3584]{1,0:T(8,128)(2,1)S(1)}, bf16[32,3584]{1,0:T(8,128)(2,1)S(1)}, u32[]{:S(2)}, u32[]{:S(2)}) collective-permute-start(bf16[32,3584]{1,0:T(8,128)(2,1)S(1)} %shard_map.83), channel_id=1, source_target_pairs={{0,2},{1,3},{2,0},{3,1},{4,6},{5,7},{6,4},{7,5},{8,10},{9,11},{10,... | collective-permute-start | bytes 688136 | tf_op jit(solution)/shard_map/ppermute | solution.py:266
  24.9 13.3 %collective-permute-start.5 = (bf16[32,3712]{1,0:T(8,128)(2,1)S(1)}, bf16[32,3712]{1,0:T(8,128)(2,1)S(1)}, u32[]{:S(2)}, u32[]{:S(2)}) collective-permute-start(bf16[32,3712]{1,0:T(8,128)(2,1)S(1)} %collective-permute-done.2.outer_x.inner_x), channel_id=1, source_target_pairs={{2,4},{3,5},{4,2},{5,3},{0,1},{1,0},{6,7},{7,6},{10,12},{11,13},{1... | collective-permute-start | bytes 712712 | tf_op jit(solution)/shard_map/ppermute | solution.py:266
  24.9 13.2 %collective-permute-start.4 = (bf16[32,3712]{1,0:T(8,128)(2,1)S(1)}, bf16[32,3712]{1,0:T(8,128)(2,1)S(1)}, u32[]{:S(2)}, u32[]{:S(2)}) collective-permute-start(bf16[32,3712]{1,0:T(8,128)(2,1)S(1)} %shard_map.78), channel_id=1, source_target_pairs={{0,2},{1,3},{2,0},{3,1},{4,6},{5,7},{6,4},{7,5},{8,10},{9,11},{10,... | collective-permute-start | bytes 712712 | tf_op jit(solution)/shard_map/ppermute | solution.py:266
  39.3 11.6 %collective-permute-start.10 = (bf16[32,3712]{1,0:T(8,128)(2,1)S(1)}, bf16[32,3712]{1,0:T(8,128)(2,1)S(1)}, u32[]{:S(2)}, u32[]{:S(2)}) collective-permute-start(bf16[32,3712]{1,0:T(8,128)(2,1)S(1)} %collective-permute-done.4.outer_x.inner_x), channel_id=1, source_target_pairs={{2,4},{3,5},{4,2},{5,3},{0,1},{1,0},{6,7},{7,6},{10,12},{11,13},{1... | collective-permute-start | bytes 712712 | tf_op jit(solution)/shard_map/ppermute | solution.py:266
  40.5 10.4 %collective-permute-start.9 = (bf16[32,3712]{1,0:T(8,128)(2,1)S(1)}, bf16[32,3712]{1,0:T(8,128)(2,1)S(1)}, u32[]{:S(2)}, u32[]{:S(2)}) collective-permute-start(bf16[32,3712]{1,0:T(8,128)(2,1)S(1)} %shard_map.82), channel_id=1, source_target_pairs={{0,2},{1,3},{2,0},{3,1},{4,6},{5,7},{6,4},{7,5},{8,10},{9,11},{10,... | collective-permute-start | bytes 712712 | tf_op jit(solution)/shard_map/ppermute | solution.py:266
  41.4 11.9 %collective-permute-start.19 = (bf16[32,3584]{1,0:T(8,128)(2,1)S(1)}, bf16[32,3584]{1,0:T(8,128)(2,1)S(1)}, u32[]{:S(2)}, u32[]{:S(2)}) collective-permute-start(bf16[32,3584]{1,0:T(8,128)(2,1)S(1)} %shard_map.88), channel_id=1, source_target_pairs={{0,2},{1,3},{2,0},{3,1},{4,6},{5,7},{6,4},{7,5},{8,10},{9,11},{10,... | collective-permute-start | bytes 688136 | tf_op jit(solution)/shard_map/ppermute | solution.py:266
  53.4 9.9 %collective-permute-start.20 = (bf16[64,3712]{1,0:T(8,128)(2,1)S(1)}, bf16[64,3712]{1,0:T(8,128)(2,1)S(1)}, u32[]{:S(2)}, u32[]{:S(2)}) collective-permute-start(bf16[64,3712]{1,0:T(8,128)(2,1)S(1)} %shard_map.90.block), channel_id=1, source_target_pairs={{0,1},{1,0},{2,3},{3,2},{4,5},{5,4},{6,7},{7,6},{8,9},{9,8},{10,11... | collective-permute-start | bytes 1425416 | tf_op jit(solution)/shard_map/ppermute | solution.py:266
  54.5 12.1 %collective-permute-start.16 = (bf16[32,3712]{1,0:T(8,128)(2,1)S(1)}, bf16[32,3712]{1,0:T(8,128)(2,1)S(1)}, u32[]{:S(2)}, u32[]{:S(2)}) collective-permute-start(bf16[32,3712]{1,0:T(8,128)(2,1)S(1)} %get-tuple-element.63.mine.passed), channel_id=1, source_target_pairs={{2,4},{3,5},{4,2},{5,3},{0,1},{1,0},{6,7},{7,6},{10,12},{11,13},{1... | collective-permute-start | bytes 712712 | tf_op jit(solution)/shard_map/ppermute | solution.py:266
  55.7 10.9 %collective-permute-start.15 = (bf16[32,3712]{1,0:T(8,128)(2,1)S(1)}, bf16[32,3712]{1,0:T(8,128)(2,1)S(1)}, u32[]{:S(2)}, u32[]{:S(2)}) collective-permute-start(bf16[32,3712]{1,0:T(8,128)(2,1)S(1)} %shard_map.87), channel_id=1, source_target_pairs={{0,2},{1,3},{2,0},{3,1},{4,6},{5,7},{6,4},{7,5},{8,10},{9,11},{10,... | collective-permute-start | bytes 712712 | tf_op jit(solution)/shard_map/ppermute | solution.py:266
  57.0 11.5 %collective-permute-start.26 = (bf16[32,3584]{1,0:T(8,128)(2,1)S(1)}, bf16[32,3584]{1,0:T(8,128)(2,1)S(1)}, u32[]{:S(2)}, u32[]{:S(2)}) collective-permute-start(bf16[32,3584]{1,0:T(8,128)(2,1)S(1)} %shard_map.94), channel_id=1, source_target_pairs={{0,2},{1,3},{2,0},{3,1},{4,6},{5,7},{6,4},{7,5},{8,10},{9,11},{10,... | collective-permute-start | bytes 688136 | tf_op jit(solution)/shard_map/ppermute | solution.py:266
  68.7 10.4 %collective-permute-start.27 = (bf16[64,3712]{1,0:T(8,128)(2,1)S(1)}, bf16[64,3712]{1,0:T(8,128)(2,1)S(1)}, u32[]{:S(2)}, u32[]{:S(2)}) collective-permute-start(bf16[64,3712]{1,0:T(8,128)(2,1)S(1)} %shard_map.96.block), channel_id=1, source_target_pairs={{0,1},{1,0},{2,3},{3,2},{4,5},{5,4},{6,7},{7,6},{8,9},{9,8},{10,11... | collective-permute-start | bytes 1425416 | tf_op jit(solution)/shard_map/ppermute | solution.py:266
  71.0 11.3 %collective-permute-start.22 = (bf16[32,3712]{1,0:T(8,128)(2,1)S(1)}, bf16[32,3712]{1,0:T(8,128)(2,1)S(1)}, u32[]{:S(2)}, u32[]{:S(2)}) collective-permute-start(bf16[32,3712]{1,0:T(8,128)(2,1)S(1)} %shard_map.92), channel_id=1, source_target_pairs={{0,2},{1,3},{2,0},{3,1},{4,6},{5,7},{6,4},{7,5},{8,10},{9,11},{10,... | collective-permute-start | bytes 712712 | tf_op jit(solution)/shard_map/ppermute | solution.py:266
  72.6 11.2 %collective-permute-start.33 = (bf16[32,3584]{1,0:T(8,128)(2,1)S(1)}, bf16[32,3584]{1,0:T(8,128)(2,1)S(1)}, u32[]{:S(2)}, u32[]{:S(2)}) collective-permute-start(bf16[32,3584]{1,0:T(8,128)(2,1)S(1)} %shard_map.100), channel_id=1, source_target_pairs={{0,2},{1,3},{2,0},{3,1},{4,6},{5,7},{6,4},{7,5},{8,10},{9,11},{10,... | collective-permute-start | bytes 688136 | tf_op jit(solution)/shard_map/ppermute | solution.py:266
  87.9 11.1 %collective-permute-start.39 = (bf16[32,3584]{1,0:T(8,128)(2,1)S(1)}, bf16[32,3584]{1,0:T(8,128)(2,1)S(1)}, u32[]{:S(2)}, u32[]{:S(2)}) collective-permute-start(bf16[32,3584]{1,0:T(8,128)(2,1)S(1)} %shard_map.106), channel_id=1, source_target_pairs={{0,2},{1,3},{2,0},{3,1},{4,6},{5,7},{6,4},{7,5},{8,10},{9,11},{10,... | collective-permute-start | bytes 688136 | tf_op jit(solution)/shard_map/ppermute | solution.py:266
  99.8 15.3 %collective-permute-start.52 = (bf16[64,3712]{1,0:T(8,128)(2,1)S(1)}, bf16[64,3712]{1,0:T(8,128)(2,1)S(1)}, u32[]{:S(2)}, u32[]{:S(2)}) collective-permute-start(bf16[64,3712]{1,0:T(8,128)(2,1)S(1)} %get-tuple-element.104.block), channel_id=1, source_target_pairs={{0,1},{1,0},{2,3},{3,2},{4,5},{5,4},{6,7},{7,6},{8,9},{9,8},{10,11... | collective-permute-start | bytes 1425416 | tf_op jit(solution)/shard_map/ppermute | solution.py:266
  99.8 15.4 %collective-permute-start = (bf16[64,3712]{1,0:T(8,128)(2,1)S(1)}, bf16[64,3712]{1,0:T(8,128)(2,1)S(1)}, u32[]{:S(2)}, u32[]{:S(2)}) collective-permute-start(bf16[64,3712]{1,0:T(8,128)(2,1)S(1)} %get-tuple-element.58.block), channel_id=1, source_target_pairs={{0,1},{1,0},{2,3},{3,2},{4,5},{5,4},{6,7},{7,6},{8,9},{9,8},{10,11... | collective-permute-start | bytes 1425416 | tf_op jit(solution)/shard_map/ppermute | solution.py:266
  102.9 18.7 %collective-permute-start.42 = (bf16[32,3584]{1,0:T(8,128)(2,1)S(1)}, bf16[32,3584]{1,0:T(8,128)(2,1)S(1)}, u32[]{:S(2)}, u32[]{:S(2)}) collective-permute-start(bf16[32,3584]{1,0:T(8,128)(2,1)S(1)} %shard_map.110), channel_id=1, source_target_pairs={{2,4},{3,5},{4,2},{5,3},{0,1},{1,0},{6,7},{7,6},{10,12},{11,13},{1... | collective-permute-start | bytes 688136 | tf_op jit(solution)/shard_map/ppermute | solution.py:266
  103.3 19.0 %collective-permute-start.37 = (bf16[32,3584]{1,0:T(8,128)(2,1)S(1)}, bf16[32,3584]{1,0:T(8,128)(2,1)S(1)}, u32[]{:S(2)}, u32[]{:S(2)}) collective-permute-start(bf16[32,3584]{1,0:T(8,128)(2,1)S(1)} %shard_map.105), channel_id=1, source_target_pairs={{2,4},{3,5},{4,2},{5,3},{0,1},{1,0},{6,7},{7,6},{10,12},{11,13},{1... | collective-permute-start | bytes 688136 | tf_op jit(solution)/shard_map/ppermute | solution.py:266
  103.9 18.5 %collective-permute-start.46 = (bf16[32,3584]{1,0:T(8,128)(2,1)S(1)}, bf16[32,3584]{1,0:T(8,128)(2,1)S(1)}, u32[]{:S(2)}, u32[]{:S(2)}) collective-permute-start(bf16[32,3584]{1,0:T(8,128)(2,1)S(1)} %shard_map.113), channel_id=1, source_target_pairs={{0,2},{1,3},{2,0},{3,1},{4,6},{5,7},{6,4},{7,5},{8,10},{9,11},{10,... | collective-permute-start | bytes 688136 | tf_op jit(solution)/shard_map/ppermute | solution.py:266
  123.7 10.8 %collective-permute-start.51 = (bf16[32,3584]{1,0:T(8,128)(2,1)S(1)}, bf16[32,3584]{1,0:T(8,128)(2,1)S(1)}, u32[]{:S(2)}, u32[]{:S(2)}) collective-permute-start(bf16[32,3584]{1,0:T(8,128)(2,1)S(1)} %shard_map.116), channel_id=1, source_target_pairs={{2,4},{3,5},{4,2},{5,3},{0,1},{1,0},{6,7},{7,6},{10,12},{11,13},{1... | collective-permute-start | bytes 688136 | tf_op jit(solution)/shard_map/ppermute | solution.py:266
  123.9 10.5 %collective-permute-start.50 = (bf16[32,3584]{1,0:T(8,128)(2,1)S(1)}, bf16[32,3584]{1,0:T(8,128)(2,1)S(1)}, u32[]{:S(2)}, u32[]{:S(2)}) collective-permute-start(bf16[32,3584]{1,0:T(8,128)(2,1)S(1)} %shard_map.115), channel_id=1, source_target_pairs={{0,2},{1,3},{2,0},{3,1},{4,6},{5,7},{6,4},{7,5},{8,10},{9,11},{10,... | collective-permute-start | bytes 688136 | tf_op jit(solution)/shard_map/ppermute | solution.py:266
  128.0 10.2 %collective-permute-start.43 = (bf16[32,3584]{1,0:T(8,128)(2,1)S(1)}, bf16[32,3584]{1,0:T(8,128)(2,1)S(1)}, u32[]{:S(2)}, u32[]{:S(2)}) collective-permute-start(bf16[32,3584]{1,0:T(8,128)(2,1)S(1)} %shard_map.111), channel_id=1, source_target_pairs={{0,2},{1,3},{2,0},{3,1},{4,6},{5,7},{6,4},{7,5},{8,10},{9,11},{10,... | collective-permute-start | bytes 688136 | tf_op jit(solution)/shard_map/ppermute | solution.py:266
  (32 other events, 147.6 us)

commit v4 on v3

--- a/solution.py
+++ b/solution.py
@@ -144,6 +144,20 @@
         copy.wait()
 
 
+def rest_kernel(devices, part, starts, gate_hbm, up_hbm, *refs):
+    given, refs = refs[:5], refs[5:]
+    outs, (gate_w, up_w), scratch, load_sems = refs[: len(starts)], refs[len(starts) : -5], refs[-5:-1], refs[-1]
+    copies = [
+        pltpu.make_async_copy(gate_hbm.at[0], gate_w, load_sems.at[0]),
+        pltpu.make_async_copy(up_hbm.at[0], up_w, load_sems.at[1]),
+    ]
+    for copy in copies:
+        copy.start()
+    prepare_kernel(devices, part, starts, *given, *outs, *scratch)
+    for copy in copies:
+        copy.wait()
+
+
 def gate_kernel(before, out):
     out[...] = before[...]
 
@@ -268,23 +282,30 @@
     long = width + LANES
     given = [pltpu.with_memory_space_constraint(v, pltpu.HBM) for v in (placed, tokens, expert_ids.T, gate_probs.T)]
 
-    def prepare(pieces, after):
+    def prepare(pieces, after, *weights):
         starts = [first for first, _, _ in pieces]
+        kernel = rest_kernel if weights else prepare_kernel
+        loaded = [pltpu.VMEM(w.shape[1:], w.dtype) for w in weights]
+        sources = [pltpu.with_memory_space_constraint(w, pltpu.HBM) for w in weights]
         return pl.pallas_call(
-            functools.partial(prepare_kernel, devices, part, starts),
-            in_specs=[pl.BlockSpec(memory_space=pltpu.HBM)] * 4 + [pl.BlockSpec(memory_space=pl.ANY)],
-            out_specs=[vmem] * len(pieces),
-            out_shape=[jax.ShapeDtypeStruct(shape, jnp.bfloat16) for _, *shape in pieces],
+            functools.partial(kernel, devices, part, starts),
+            in_specs=[pl.BlockSpec(memory_space=pltpu.HBM)] * (4 + len(weights)) + [pl.BlockSpec(memory_space=pl.ANY)],
+            out_specs=[vmem] * (len(pieces) + len(weights)),
+            out_shape=[jax.ShapeDtypeStruct(shape, jnp.bfloat16) for _, *shape in pieces] + loaded,
             scratch_shapes=[pltpu.SMEM(placed.shape, placed.dtype)]
             + [pltpu.VMEM(v.shape, v.dtype) for v in given[2:]]
-            + [pltpu.SemaphoreType.DMA((3 + len(pieces),))],
+            + [pltpu.SemaphoreType.DMA((3 + len(pieces),))]
+            + [pltpu.SemaphoreType.DMA((2,))] * bool(weights),
+            cost_estimate=pl.CostEstimate(flops=w_gate.size * 400, bytes_accessed=0, transcendentals=0)
+            if weights
+            else None,
             compiler_params=pltpu.CompilerParams(vmem_limit_bytes=4 << 20),
-        )(*given, after)
+        )(*sources, *given, after)
 
     own_a = prepare([(0, part, long), (part, part, width)], given[0])
     others = [(half, part, long), (half + part, part, width), (0, half, long), (half, half, long)]
-    own_b = prepare(others, own_a[0])
-    own_b, own_whole = own_b[:2], own_b[2:]
+    made = prepare(others, own_a[0], w_gate, w_up)
+    own_b, own_whole, held = made[:2], made[2:4], list(made[4:])
 
     hbm = pl.BlockSpec(memory_space=pltpu.HBM)
 
@@ -302,7 +323,6 @@
             compiler_params=pltpu.CompilerParams(vmem_limit_bytes=1 << 20),
         )(*[pltpu.with_memory_space_constraint(w, pltpu.HBM) for w in sources], after)
 
-    held = load((w_gate, w_up), own_a[0])
     held += load((w_down,), own_a[0])
 
     def run(block):

time: 141 us -> 140 us (level)
  waiting for transfers between devices: 30.1 us -> 35.2 us
  starting transfers between devices: 67.3 us -> 62.6 us
    pallas_call x2 -> x1, Pallas kernels: 8.28 us -> 3.09 us  [load(): pl.pallas_call(functools.partial(load_kernel, count), in_specs=[hbm] * co...]
    ppermute x56, waiting for transfers between devices: 30.1 us -> 35.2 us  [send(): return lax.ppermute(value, 'exp', perm)]
    ppermute x56, starting transfers between devices: 67.3 us -> 62.6 us  [send(): return lax.ppermute(value, 'exp', perm)]
    pallas_call x2, Pallas kernels: 2.6 us -> 6.79 us  [prepare(): pl.pallas_call(functools.partial(kernel, devices, part, starts), in_specs...]
  transfers between devices with their start and end apart: 56 -> 56, of which waited for: 16 -> 17; matrix products, arithmetic and copies ran while one was open for 0% -> 0% of each run, Pallas kernels for 28% -> 27%
where the time goes in v4:
time: 140 us; the launch traced here: 139 us
  starting transfers between devices  62.6 us (45%)
  Pallas kernels  40.1 us (29%)
  waiting for transfers between devices  35.2 us (25%)
    ppermute x56, starting transfers between devices, send(): return lax.ppermute(value, 'exp', perm)  62.6 us
    ppermute x56, waiting for transfers between devices, send(): return lax.ppermute(value, 'exp', perm)  35.2 us
    pallas_call x8, Pallas kernels, run(): mine, other_x, other_y = call(spot, block, twin, *held)  25.5 us
    pallas_call x2, Pallas kernels, prepare(): pl.pallas_call(functools.partial(kernel, devices, part, starts), in_specs...  6.79 us
    pallas_call x1, Pallas kernels, load(): pl.pallas_call(functools.partial(load_kernel, count), in_specs=[hbm] * co...  3.09 us
  transfers between devices with their start and end apart: 56, of which 17 were waited for; matrix products, arithmetic and copies ran while one was open for 0% of the time, Pallas kernels for 27%

profile of v4, /device:TPU:0, one launch (start us, length us, event | category | flops | bytes accessed | tf_op | source)
XLA Modules:
  0.0 138.7 jit_solution(6761962533740049013)
XLA Ops:
  1.7 4.1 %collective-permute-start.2 = (bf16[32,3712]{1,0:T(8,128)(2,1)S(1)}, bf16[32,3712]{1,0:T(8,128)(2,1)S(1)}, u32[]{:S(2)}, u32[]{:S(2)}) collective-permute-start(bf16[32,3712]{1,0:T(8,128)(2,1)S(1)} %get-tuple-element.57.refs_4_.refs_1_), channel_id=1, source_target_pairs={{0,2},{1,3},{2,0},{3,1},{4,6},{5,7},{6,4},{7,5},{8,10},{9,11},{10,... | collective-permute-start | bytes 712712 | tf_op jit(solution)/shard_map/ppermute | solution.py:280
  5.9 6.6 %collective-permute-done.2.outer_x.inner_x = bf16[32,3712]{1,0:T(8,128)(2,1)S(1)} collective-permute-done((bf16[32,3712]{1,0:T(8,128)(2,1)S(1)}, bf16[32,3712]{1,0:T(8,128)(2,1)S(1)}, u32[]{:S(2)}, u32[]{:S(2)}) %collective-permute-start.2) | collective-permute-done | bytes 237600 | tf_op jit(solution)/shard_map/ppermute | solution.py:280
  12.5 3.8 %collective-permute-done.6.outer_y.inner_y = bf16[32,3584]{1,0:T(8,128)(2,1)S(1)} collective-permute-done((bf16[32,3584]{1,0:T(8,128)(2,1)S(1)}, bf16[32,3584]{1,0:T(8,128)(2,1)S(1)}, u32[]{:S(2)}, u32[]{:S(2)}) %collective-permute-start.6) | collective-permute-done | bytes 229408 | tf_op jit(solution)/shard_map/ppermute | solution.py:280
  16.9 5.7 %shard_map.74 = (bf16[32,3712]{1,0:T(8,128)(2,1)S(1)}, bf16[32,3584]{1,0:T(8,128)(2,1)S(1)}, bf16[64,3712]{1,0:T(8,128)(2,1)S(1)}, bf16[64,3712]{1,0:T(8,128)(2,...) custom-call(bf16[1,3584,1024]{2,1,0:T(8,128)(2,1)} %gate_hbm.1, bf16[1,3584,1024]{2,1,0:T(8,128)(2,1)} %up_hbm.1, ...), custom_call_target="tpu_custom_call" | custom-call | flops 1468006400 | tf_op jit(solution)/shard_map/pallas_call | solution.py:290
  22.7 3.3 %collective-permute-start.4 = (bf16[32,3712]{1,0:T(8,128)(2,1)S(1)}, bf16[32,3712]{1,0:T(8,128)(2,1)S(1)}, u32[]{:S(2)}, u32[]{:S(2)}) collective-permute-start(bf16[32,3712]{1,0:T(8,128)(2,1)S(1)} %shard_map.77), channel_id=1, source_target_pairs={{0,2},{1,3},{2,0},{3,1},{4,6},{5,7},{6,4},{7,5},{8,10},{9,11},{10,... | collective-permute-start | bytes 712712 | tf_op jit(solution)/shard_map/ppermute | solution.py:280
  26.2 3.1 %shard_map.75.down_w = bf16[1024,3584]{1,0:T(8,128)(2,1)S(1)} custom-call(bf16[1,1024,3584]{2,1,0:T(8,128)(2,1)} %refs_0_.3, bf16[32,3712]{1,0:T(8,128)(2,1)S(1)} %get-tuple-element.57.refs_4_.refs_1_), custom_call_target="tpu_custom_call" | custom-call | flops 734003200 | tf_op jit(solution)/shard_map/pallas_call | solution.py:314
  29.3 3.2 %shard_map.80 = (f32[64,3584]{1,0:T(8,128)S(1)}, bf16[32,3584]{1,0:T(8,128)(2,1)S(1)}, bf16[32,3584]{1,0:T(8,128)(2,1)S(1)}) custom-call(s32[1]{0:T(128)} %bitcast.spot, bf16[64,3712]{1,0:T(8,128)(2,1)S(1)} %shard_map.79.block, bf16[64,3712]{1,0:T(8,128)(2,1)S(1)} %collective-permute-done.7.twin, bf16[3584,1024]{1,0:T(8,128)(2,1)S(1)} %get-tuple-element.59.gate_w, ...), custom_call_target="tpu_custom_call" | custom-call | flops 704643072 | tf_op jit(solution)/shard_map/pallas_call | solution.py:343
  32.6 4.1 %collective-permute-done.12.outer_y.inner_y = bf16[32,3584]{1,0:T(8,128)(2,1)S(1)} collective-permute-done((bf16[32,3584]{1,0:T(8,128)(2,1)S(1)}, bf16[32,3584]{1,0:T(8,128)(2,1)S(1)}, u32[]{:S(2)}, u32[]{:S(2)}) %collective-permute-start.12) | collective-permute-done | bytes 229408 | tf_op jit(solution)/shard_map/ppermute | solution.py:280
  41.3 6.4 %collective-permute-start.19 = (bf16[32,3584]{1,0:T(8,128)(2,1)S(1)}, bf16[32,3584]{1,0:T(8,128)(2,1)S(1)}, u32[]{:S(2)}, u32[]{:S(2)}) collective-permute-start(bf16[32,3584]{1,0:T(8,128)(2,1)S(1)} %shard_map.87), channel_id=1, source_target_pairs={{0,2},{1,3},{2,0},{3,1},{4,6},{5,7},{6,4},{7,5},{8,10},{9,11},{10,... | collective-permute-start | bytes 688136 | tf_op jit(solution)/shard_map/ppermute | solution.py:280
  47.7 3.2 %shard_map.85 = (f32[64,3584]{1,0:T(8,128)S(1)}, bf16[32,3584]{1,0:T(8,128)(2,1)S(1)}, bf16[32,3584]{1,0:T(8,128)(2,1)S(1)}) custom-call(s32[1]{0:T(128)} %bitcast.spot, bf16[64,3712]{1,0:T(8,128)(2,1)S(1)} %shard_map.84.block, bf16[64,3712]{1,0:T(8,128)(2,1)S(1)} %collective-permute-done.13.twin, bf16[3584,1024]{1,0:T(8,128)(2,1)S(1)} %get-tuple-element.59.gate_w, ...), custom_call_target="tpu_custom_call" | custom-call | flops 704643072 | tf_op jit(solution)/shard_map/pallas_call | solution.py:343
  56.9 6.4 %collective-permute-start.26 = (bf16[32,3584]{1,0:T(8,128)(2,1)S(1)}, bf16[32,3584]{1,0:T(8,128)(2,1)S(1)}, u32[]{:S(2)}, u32[]{:S(2)}) collective-permute-start(bf16[32,3584]{1,0:T(8,128)(2,1)S(1)} %shard_map.93), channel_id=1, source_target_pairs={{0,2},{1,3},{2,0},{3,1},{4,6},{5,7},{6,4},{7,5},{8,10},{9,11},{10,... | collective-permute-start | bytes 688136 | tf_op jit(solution)/shard_map/ppermute | solution.py:280
  63.2 3.2 %shard_map.90 = (f32[64,3584]{1,0:T(8,128)S(1)}, bf16[32,3584]{1,0:T(8,128)(2,1)S(1)}, bf16[32,3584]{1,0:T(8,128)(2,1)S(1)}) custom-call(s32[1]{0:T(128)} %bitcast.spot, bf16[64,3712]{1,0:T(8,128)(2,1)S(1)} %shard_map.89.block, bf16[64,3712]{1,0:T(8,128)(2,1)S(1)} %collective-permute-done.20.twin, bf16[3584,1024]{1,0:T(8,128)(2,1)S(1)} %get-tuple-element.59.gate_w, ...), custom_call_target="tpu_custom_call" | custom-call | flops 704643072 | tf_op jit(solution)/shard_map/pallas_call | solution.py:343
  72.4 6.6 %collective-permute-start.33 = (bf16[32,3584]{1,0:T(8,128)(2,1)S(1)}, bf16[32,3584]{1,0:T(8,128)(2,1)S(1)}, u32[]{:S(2)}, u32[]{:S(2)}) collective-permute-start(bf16[32,3584]{1,0:T(8,128)(2,1)S(1)} %shard_map.99), channel_id=1, source_target_pairs={{0,2},{1,3},{2,0},{3,1},{4,6},{5,7},{6,4},{7,5},{8,10},{9,11},{10,... | collective-permute-start | bytes 688136 | tf_op jit(solution)/shard_map/ppermute | solution.py:280
  79.0 3.2 %shard_map.96 = (f32[64,3584]{1,0:T(8,128)S(1)}, bf16[32,3584]{1,0:T(8,128)(2,1)S(1)}, bf16[32,3584]{1,0:T(8,128)(2,1)S(1)}) custom-call(s32[1]{0:T(128)} %bitcast.spot, bf16[64,3712]{1,0:T(8,128)(2,1)S(1)} %shard_map.95.block, bf16[64,3712]{1,0:T(8,128)(2,1)S(1)} %collective-permute-done.27.twin, bf16[3584,1024]{1,0:T(8,128)(2,1)S(1)} %get-tuple-element.59.gate_w, ...), custom_call_target="tpu_custom_call" | custom-call | flops 704643072 | tf_op jit(solution)/shard_map/pallas_call | solution.py:343
  88.7 3.2 %shard_map.102 = (f32[64,3584]{1,0:T(8,128)S(1)}, bf16[32,3584]{1,0:T(8,128)(2,1)S(1)}, bf16[32,3584]{1,0:T(8,128)(2,1)S(1)}) custom-call(s32[1]{0:T(128)} %bitcast.spot, bf16[64,3712]{1,0:T(8,128)(2,1)S(1)} %shard_map.101.block, bf16[64,3712]{1,0:T(8,128)(2,1)S(1)} %collective-permute-done.34.twin, bf16[3584,1024]{1,0:T(8,128)(2,1)S(1)} %get-tuple-element.59.gate_w, ...), custom_call_target="tpu_custom_call" | custom-call | flops 704643072 | tf_op jit(solution)/shard_map/pallas_call | solution.py:343
  91.9 2.4 %collective-permute-done.29.other.outer_x = bf16[32,3712]{1,0:T(8,128)(2,1)S(1)} collective-permute-done((bf16[32,3712]{1,0:T(8,128)(2,1)S(1)}, bf16[32,3712]{1,0:T(8,128)(2,1)S(1)}, u32[]{:S(2)}, u32[]{:S(2)}) %collective-permute-start.29) | collective-permute-done | bytes 237600 | tf_op jit(solution)/shard_map/ppermute | solution.py:280
  94.3 4.1 %collective-permute-done.39.outer_y.other = bf16[32,3584]{1,0:T(8,128)(2,1)S(1)} collective-permute-done((bf16[32,3584]{1,0:T(8,128)(2,1)S(1)}, bf16[32,3584]{1,0:T(8,128)(2,1)S(1)}, u32[]{:S(2)}, u32[]{:S(2)}) %collective-permute-start.39) | collective-permute-done | bytes 229408 | tf_op jit(solution)/shard_map/ppermute | solution.py:280
  103.1 8.2 %collective-permute-start.36 = (bf16[32,3584]{1,0:T(8,128)(2,1)S(1)}, bf16[32,3584]{1,0:T(8,128)(2,1)S(1)}, u32[]{:S(2)}, u32[]{:S(2)}) collective-permute-start(bf16[32,3584]{1,0:T(8,128)(2,1)S(1)} %shard_map.103), channel_id=1, source_target_pairs={{0,2},{1,3},{2,0},{3,1},{4,6},{5,7},{6,4},{7,5},{8,10},{9,11},{10,... | collective-permute-start | bytes 688136 | tf_op jit(solution)/shard_map/ppermute | solution.py:280
  111.4 3.2 %shard_map.108 = (f32[64,3584]{1,0:T(8,128)S(1)}, bf16[32,3584]{1,0:T(8,128)(2,1)S(1)}, bf16[32,3584]{1,0:T(8,128)(2,1)S(1)}) custom-call(s32[1]{0:T(128)} %bitcast.spot, bf16[64,3712]{1,0:T(8,128)(2,1)S(1)} %shard_map.107.block, bf16[64,3712]{1,0:T(8,128)(2,1)S(1)} %collective-permute-done.40.twin, bf16[3584,1024]{1,0:T(8,128)(2,1)S(1)} %get-tuple-element.59.gate_w, ...), custom_call_target="tpu_custom_call" | custom-call | flops 704643072 | tf_op jit(solution)/shard_map/pallas_call | solution.py:343
  114.7 3.2 %shard_map.76 = (f32[64,3584]{1,0:T(8,128)S(1)}, bf16[32,3584]{1,0:T(8,128)(2,1)S(1)}, bf16[32,3584]{1,0:T(8,128)(2,1)S(1)}) custom-call(s32[1]{0:T(128)} %bitcast.spot, bf16[64,3712]{1,0:T(8,128)(2,1)S(1)} %get-tuple-element.58.block, bf16[64,3712]{1,0:T(8,128)(2,1)S(1)} %collective-permute-done.twin, bf16[3584,1024]{1,0:T(8,128)(2,1)S(1)} %get-tuple-element.59.gate_w, ...), custom_call_target="tpu_custom_call" | custom-call | flops 704643072 | tf_op jit(solution)/shard_map/pallas_call | solution.py:343
  117.9 3.2 %shard_map.116 = (f32[64,3584]{1,0:T(8,128)S(1)}, bf16[32,3584]{1,0:T(8,128)(2,1)S(1)}, bf16[32,3584]{1,0:T(8,128)(2,1)S(1)}) custom-call(s32[1]{0:T(128)} %bitcast.spot, bf16[64,3712]{1,0:T(8,128)(2,1)S(1)} %get-tuple-element.104.block, bf16[64,3712]{1,0:T(8,128)(2,1)S(1)} %collective-permute-done.52.twin, bf16[3584,1024]{1,0:T(8,128)(2,1)S(1)} %get-tuple-element.59.gate_w, ...), custom_call_target="tpu_custom_call" | custom-call | flops 704643072 | tf_op jit(solution)/shard_map/pallas_call | solution.py:343
  123.4 3.6 %collective-permute-start.50 = (bf16[32,3584]{1,0:T(8,128)(2,1)S(1)}, bf16[32,3584]{1,0:T(8,128)(2,1)S(1)}, u32[]{:S(2)}, u32[]{:S(2)}) collective-permute-start(bf16[32,3584]{1,0:T(8,128)(2,1)S(1)} %shard_map.114), channel_id=1, source_target_pairs={{0,2},{1,3},{2,0},{3,1},{4,6},{5,7},{6,4},{7,5},{8,10},{9,11},{10,... | collective-permute-start | bytes 688136 | tf_op jit(solution)/shard_map/ppermute | solution.py:280
  127.5 5.4 %collective-permute-start.43 = (bf16[32,3584]{1,0:T(8,128)(2,1)S(1)}, bf16[32,3584]{1,0:T(8,128)(2,1)S(1)}, u32[]{:S(2)}, u32[]{:S(2)}) collective-permute-start(bf16[32,3584]{1,0:T(8,128)(2,1)S(1)} %shard_map.110), channel_id=1, source_target_pairs={{0,2},{1,3},{2,0},{3,1},{4,6},{5,7},{6,4},{7,5},{8,10},{9,11},{10,... | collective-permute-start | bytes 688136 | tf_op jit(solution)/shard_map/ppermute | solution.py:280
  134.7 2.9 %collective-permute-done.43.refs_1_.refs_2_ = bf16[32,3584]{1,0:T(8,128)(2,1)S(1)} collective-permute-done((bf16[32,3584]{1,0:T(8,128)(2,1)S(1)}, bf16[32,3584]{1,0:T(8,128)(2,1)S(1)}, u32[]{:S(2)}, u32[]{:S(2)}) %collective-permute-start.43) | collective-permute-done | bytes 229408 | tf_op jit(solution)/shard_map/ppermute | solution.py:280
  (138 shorter events, 35.8 us)
Async XLA Ops:
  1.7 10.8 %collective-permute-start.2 = (bf16[32,3712]{1,0:T(8,128)(2,1)S(1)}, bf16[32,3712]{1,0:T(8,128)(2,1)S(1)}, u32[]{:S(2)}, u32[]{:S(2)}) collective-permute-start(bf16[32,3712]{1,0:T(8,128)(2,1)S(1)} %get-tuple-element.57.refs_4_.refs_1_), channel_id=1, source_target_pairs={{0,2},{1,3},{2,0},{3,1},{4,6},{5,7},{6,4},{7,5},{8,10},{9,11},{10,... | collective-permute-start | bytes 712712 | tf_op jit(solution)/shard_map/ppermute | solution.py:280
  5.8 10.4 %collective-permute-start.6 = (bf16[32,3584]{1,0:T(8,128)(2,1)S(1)}, bf16[32,3584]{1,0:T(8,128)(2,1)S(1)}, u32[]{:S(2)}, u32[]{:S(2)}) collective-permute-start(bf16[32,3584]{1,0:T(8,128)(2,1)S(1)} %get-tuple-element.66), channel_id=1, source_target_pairs={{0,2},{1,3},{2,0},{3,1},{4,6},{5,7},{6,4},{7,5},{8,10},{9,11},{10,... | collective-permute-start | bytes 688136 | tf_op jit(solution)/shard_map/ppermute | solution.py:280
  16.3 13.0 %collective-permute-start.7 = (bf16[64,3712]{1,0:T(8,128)(2,1)S(1)}, bf16[64,3712]{1,0:T(8,128)(2,1)S(1)}, u32[]{:S(2)}, u32[]{:S(2)}) collective-permute-start(bf16[64,3712]{1,0:T(8,128)(2,1)S(1)} %shard_map.79.block), channel_id=1, source_target_pairs={{0,1},{1,0},{2,3},{3,2},{4,5},{5,4},{6,7},{7,6},{8,9},{9,8},{10,11... | collective-permute-start | bytes 1425416 | tf_op jit(solution)/shard_map/ppermute | solution.py:280
  26.0 10.7 %collective-permute-start.12 = (bf16[32,3584]{1,0:T(8,128)(2,1)S(1)}, bf16[32,3584]{1,0:T(8,128)(2,1)S(1)}, u32[]{:S(2)}, u32[]{:S(2)}) collective-permute-start(bf16[32,3584]{1,0:T(8,128)(2,1)S(1)} %shard_map.82), channel_id=1, source_target_pairs={{0,2},{1,3},{2,0},{3,1},{4,6},{5,7},{6,4},{7,5},{8,10},{9,11},{10,... | collective-permute-start | bytes 688136 | tf_op jit(solution)/shard_map/ppermute | solution.py:280
  36.8 10.9 %collective-permute-start.13 = (bf16[64,3712]{1,0:T(8,128)(2,1)S(1)}, bf16[64,3712]{1,0:T(8,128)(2,1)S(1)}, u32[]{:S(2)}, u32[]{:S(2)}) collective-permute-start(bf16[64,3712]{1,0:T(8,128)(2,1)S(1)} %shard_map.84.block), channel_id=1, source_target_pairs={{0,1},{1,0},{2,3},{3,2},{4,5},{5,4},{6,7},{7,6},{8,9},{9,8},{10,11... | collective-permute-start | bytes 1425416 | tf_op jit(solution)/shard_map/ppermute | solution.py:280
  37.9 13.0 %collective-permute-start.10 = (bf16[32,3712]{1,0:T(8,128)(2,1)S(1)}, bf16[32,3712]{1,0:T(8,128)(2,1)S(1)}, u32[]{:S(2)}, u32[]{:S(2)}) collective-permute-start(bf16[32,3712]{1,0:T(8,128)(2,1)S(1)} %collective-permute-done.4.outer_x.inner_x), channel_id=1, source_target_pairs={{2,4},{3,5},{4,2},{5,3},{0,1},{1,0},{6,7},{7,6},{10,12},{11,13},{1... | collective-permute-start | bytes 712712 | tf_op jit(solution)/shard_map/ppermute | solution.py:280
  39.1 11.8 %collective-permute-start.9 = (bf16[32,3712]{1,0:T(8,128)(2,1)S(1)}, bf16[32,3712]{1,0:T(8,128)(2,1)S(1)}, u32[]{:S(2)}, u32[]{:S(2)}) collective-permute-start(bf16[32,3712]{1,0:T(8,128)(2,1)S(1)} %shard_map.81), channel_id=1, source_target_pairs={{0,2},{1,3},{2,0},{3,1},{4,6},{5,7},{6,4},{7,5},{8,10},{9,11},{10,... | collective-permute-start | bytes 712712 | tf_op jit(solution)/shard_map/ppermute | solution.py:280
  41.3 11.0 %collective-permute-start.19 = (bf16[32,3584]{1,0:T(8,128)(2,1)S(1)}, bf16[32,3584]{1,0:T(8,128)(2,1)S(1)}, u32[]{:S(2)}, u32[]{:S(2)}) collective-permute-start(bf16[32,3584]{1,0:T(8,128)(2,1)S(1)} %shard_map.87), channel_id=1, source_target_pairs={{0,2},{1,3},{2,0},{3,1},{4,6},{5,7},{6,4},{7,5},{8,10},{9,11},{10,... | collective-permute-start | bytes 688136 | tf_op jit(solution)/shard_map/ppermute | solution.py:280
  52.4 10.9 %collective-permute-start.20 = (bf16[64,3712]{1,0:T(8,128)(2,1)S(1)}, bf16[64,3712]{1,0:T(8,128)(2,1)S(1)}, u32[]{:S(2)}, u32[]{:S(2)}) collective-permute-start(bf16[64,3712]{1,0:T(8,128)(2,1)S(1)} %shard_map.89.block), channel_id=1, source_target_pairs={{0,1},{1,0},{2,3},{3,2},{4,5},{5,4},{6,7},{7,6},{8,9},{9,8},{10,11... | collective-permute-start | bytes 1425416 | tf_op jit(solution)/shard_map/ppermute | solution.py:280
  53.4 13.0 %collective-permute-start.16 = (bf16[32,3712]{1,0:T(8,128)(2,1)S(1)}, bf16[32,3712]{1,0:T(8,128)(2,1)S(1)}, u32[]{:S(2)}, u32[]{:S(2)}) collective-permute-start(bf16[32,3712]{1,0:T(8,128)(2,1)S(1)} %get-tuple-element.63.mine.passed), channel_id=1, source_target_pairs={{2,4},{3,5},{4,2},{5,3},{0,1},{1,0},{6,7},{7,6},{10,12},{11,13},{1... | collective-permute-start | bytes 712712 | tf_op jit(solution)/shard_map/ppermute | solution.py:280
  54.6 11.8 %collective-permute-start.15 = (bf16[32,3712]{1,0:T(8,128)(2,1)S(1)}, bf16[32,3712]{1,0:T(8,128)(2,1)S(1)}, u32[]{:S(2)}, u32[]{:S(2)}) collective-permute-start(bf16[32,3712]{1,0:T(8,128)(2,1)S(1)} %shard_map.86), channel_id=1, source_target_pairs={{0,2},{1,3},{2,0},{3,1},{4,6},{5,7},{6,4},{7,5},{8,10},{9,11},{10,... | collective-permute-start | bytes 712712 | tf_op jit(solution)/shard_map/ppermute | solution.py:280
  56.9 11.0 %collective-permute-start.26 = (bf16[32,3584]{1,0:T(8,128)(2,1)S(1)}, bf16[32,3584]{1,0:T(8,128)(2,1)S(1)}, u32[]{:S(2)}, u32[]{:S(2)}) collective-permute-start(bf16[32,3584]{1,0:T(8,128)(2,1)S(1)} %shard_map.93), channel_id=1, source_target_pairs={{0,2},{1,3},{2,0},{3,1},{4,6},{5,7},{6,4},{7,5},{8,10},{9,11},{10,... | collective-permute-start | bytes 688136 | tf_op jit(solution)/shard_map/ppermute | solution.py:280
  68.1 10.9 %collective-permute-start.27 = (bf16[64,3712]{1,0:T(8,128)(2,1)S(1)}, bf16[64,3712]{1,0:T(8,128)(2,1)S(1)}, u32[]{:S(2)}, u32[]{:S(2)}) collective-permute-start(bf16[64,3712]{1,0:T(8,128)(2,1)S(1)} %shard_map.95.block), channel_id=1, source_target_pairs={{0,1},{1,0},{2,3},{3,2},{4,5},{5,4},{6,7},{7,6},{8,9},{9,8},{10,11... | collective-permute-start | bytes 1425416 | tf_op jit(solution)/shard_map/ppermute | solution.py:280
  70.4 11.8 %collective-permute-start.22 = (bf16[32,3712]{1,0:T(8,128)(2,1)S(1)}, bf16[32,3712]{1,0:T(8,128)(2,1)S(1)}, u32[]{:S(2)}, u32[]{:S(2)}) collective-permute-start(bf16[32,3712]{1,0:T(8,128)(2,1)S(1)} %shard_map.91), channel_id=1, source_target_pairs={{0,2},{1,3},{2,0},{3,1},{4,6},{5,7},{6,4},{7,5},{8,10},{9,11},{10,... | collective-permute-start | bytes 712712 | tf_op jit(solution)/shard_map/ppermute | solution.py:280
  72.4 10.8 %collective-permute-start.33 = (bf16[32,3584]{1,0:T(8,128)(2,1)S(1)}, bf16[32,3584]{1,0:T(8,128)(2,1)S(1)}, u32[]{:S(2)}, u32[]{:S(2)}) collective-permute-start(bf16[32,3584]{1,0:T(8,128)(2,1)S(1)} %shard_map.99), channel_id=1, source_target_pairs={{0,2},{1,3},{2,0},{3,1},{4,6},{5,7},{6,4},{7,5},{8,10},{9,11},{10,... | collective-permute-start | bytes 688136 | tf_op jit(solution)/shard_map/ppermute | solution.py:280
  87.6 10.8 %collective-permute-start.39 = (bf16[32,3584]{1,0:T(8,128)(2,1)S(1)}, bf16[32,3584]{1,0:T(8,128)(2,1)S(1)}, u32[]{:S(2)}, u32[]{:S(2)}) collective-permute-start(bf16[32,3584]{1,0:T(8,128)(2,1)S(1)} %shard_map.105), channel_id=1, source_target_pairs={{0,2},{1,3},{2,0},{3,1},{4,6},{5,7},{6,4},{7,5},{8,10},{9,11},{10,... | collective-permute-start | bytes 688136 | tf_op jit(solution)/shard_map/ppermute | solution.py:280
  99.0 15.6 %collective-permute-start = (bf16[64,3712]{1,0:T(8,128)(2,1)S(1)}, bf16[64,3712]{1,0:T(8,128)(2,1)S(1)}, u32[]{:S(2)}, u32[]{:S(2)}) collective-permute-start(bf16[64,3712]{1,0:T(8,128)(2,1)S(1)} %get-tuple-element.58.block), channel_id=1, source_target_pairs={{0,1},{1,0},{2,3},{3,2},{4,5},{5,4},{6,7},{7,6},{8,9},{9,8},{10,11... | collective-permute-start | bytes 1425416 | tf_op jit(solution)/shard_map/ppermute | solution.py:280
  99.1 15.6 %collective-permute-start.52 = (bf16[64,3712]{1,0:T(8,128)(2,1)S(1)}, bf16[64,3712]{1,0:T(8,128)(2,1)S(1)}, u32[]{:S(2)}, u32[]{:S(2)}) collective-permute-start(bf16[64,3712]{1,0:T(8,128)(2,1)S(1)} %get-tuple-element.104.block), channel_id=1, source_target_pairs={{0,1},{1,0},{2,3},{3,2},{4,5},{5,4},{6,7},{7,6},{8,9},{9,8},{10,11... | collective-permute-start | bytes 1425416 | tf_op jit(solution)/shard_map/ppermute | solution.py:280
  102.3 18.8 %collective-permute-start.42 = (bf16[32,3584]{1,0:T(8,128)(2,1)S(1)}, bf16[32,3584]{1,0:T(8,128)(2,1)S(1)}, u32[]{:S(2)}, u32[]{:S(2)}) collective-permute-start(bf16[32,3584]{1,0:T(8,128)(2,1)S(1)} %shard_map.109), channel_id=1, source_target_pairs={{2,4},{3,5},{4,2},{5,3},{0,1},{1,0},{6,7},{7,6},{10,12},{11,13},{1... | collective-permute-start | bytes 688136 | tf_op jit(solution)/shard_map/ppermute | solution.py:280
  102.6 19.1 %collective-permute-start.37 = (bf16[32,3584]{1,0:T(8,128)(2,1)S(1)}, bf16[32,3584]{1,0:T(8,128)(2,1)S(1)}, u32[]{:S(2)}, u32[]{:S(2)}) collective-permute-start(bf16[32,3584]{1,0:T(8,128)(2,1)S(1)} %shard_map.104), channel_id=1, source_target_pairs={{2,4},{3,5},{4,2},{5,3},{0,1},{1,0},{6,7},{7,6},{10,12},{11,13},{1... | collective-permute-start | bytes 688136 | tf_op jit(solution)/shard_map/ppermute | solution.py:280
  103.1 18.8 %collective-permute-start.36 = (bf16[32,3584]{1,0:T(8,128)(2,1)S(1)}, bf16[32,3584]{1,0:T(8,128)(2,1)S(1)}, u32[]{:S(2)}, u32[]{:S(2)}) collective-permute-start(bf16[32,3584]{1,0:T(8,128)(2,1)S(1)} %shard_map.103), channel_id=1, source_target_pairs={{0,2},{1,3},{2,0},{3,1},{4,6},{5,7},{6,4},{7,5},{8,10},{9,11},{10,... | collective-permute-start | bytes 688136 | tf_op jit(solution)/shard_map/ppermute | solution.py:280
  123.2 10.7 %collective-permute-start.51 = (bf16[32,3584]{1,0:T(8,128)(2,1)S(1)}, bf16[32,3584]{1,0:T(8,128)(2,1)S(1)}, u32[]{:S(2)}, u32[]{:S(2)}) collective-permute-start(bf16[32,3584]{1,0:T(8,128)(2,1)S(1)} %shard_map.115), channel_id=1, source_target_pairs={{2,4},{3,5},{4,2},{5,3},{0,1},{1,0},{6,7},{7,6},{10,12},{11,13},{1... | collective-permute-start | bytes 688136 | tf_op jit(solution)/shard_map/ppermute | solution.py:280
  123.4 10.5 %collective-permute-start.50 = (bf16[32,3584]{1,0:T(8,128)(2,1)S(1)}, bf16[32,3584]{1,0:T(8,128)(2,1)S(1)}, u32[]{:S(2)}, u32[]{:S(2)}) collective-permute-start(bf16[32,3584]{1,0:T(8,128)(2,1)S(1)} %shard_map.114), channel_id=1, source_target_pairs={{0,2},{1,3},{2,0},{3,1},{4,6},{5,7},{6,4},{7,5},{8,10},{9,11},{10,... | collective-permute-start | bytes 688136 | tf_op jit(solution)/shard_map/ppermute | solution.py:280
  127.5 10.2 %collective-permute-start.43 = (bf16[32,3584]{1,0:T(8,128)(2,1)S(1)}, bf16[32,3584]{1,0:T(8,128)(2,1)S(1)}, u32[]{:S(2)}, u32[]{:S(2)}) collective-permute-start(bf16[32,3584]{1,0:T(8,128)(2,1)S(1)} %shard_map.110), channel_id=1, source_target_pairs={{0,2},{1,3},{2,0},{3,1},{4,6},{5,7},{6,4},{7,5},{8,10},{9,11},{10,... | collective-permute-start | bytes 688136 | tf_op jit(solution)/shard_map/ppermute | solution.py:280
  (32 other events, 158.7 us)
